TPU v7x, 16 devices: a whole 2x2x2 slice. The times are simulated.
16 devices in a mesh: ez: 2 (over z), ey: 2 (over y), ex: 4 (over x, core).
Axes of the slice: x: 2, y: 2, z: 2, core: 2. Of those that a mesh axis runs over, the one named last changes fastest.
Arguments:
- x_tokens: bfloat16 [8192, 1024], P(('ez', 'ey', 'ex'))
- expert_ids: int32 [8192, 8], P(('ez', 'ey', 'ex'))
- gate_vals: float32 [8192, 8], P(('ez', 'ey', 'ex'))
- w_gate: bfloat16 [32, 1024, 512], P(('ex', 'ey', 'ez'))
- w_up: bfloat16 [32, 1024, 512], P(('ex', 'ey', 'ez'))
- w_down: bfloat16 [32, 512, 1024], P(('ex', 'ey', 'ez'))
Outputs:
- output: bfloat16 [8192, 1024], P(('ez', 'ey', 'ex'))
All inputs are finite; a program needn't handle non-finite values.
Results may differ from a plain program's by a relative error of at most 0.001.
Values are sent between devices in bfloat16 or wider.
A program may use at most 1 GiB of HBM per device.

v0:
```python
import jax
import jax.numpy as jnp
from jax import lax
from jax.sharding import PartitionSpec as P

TOKEN_AXES = ('ez', 'ey', 'ex')
EXPERT_AXES = ('ex', 'ey', 'ez')


def slot_layout(ids_local, n_exp, cap_slot):
    tok_dev, top_k = ids_local.shape
    flat_ids = ids_local.reshape(-1)
    match_mat = (flat_ids[:, None] == jnp.arange(n_exp)[None, :]).astype(jnp.int32)
    slot_rank = jnp.sum(jnp.cumsum(match_mat, axis=0) * match_mat, axis=1) - 1
    slot_idx = flat_ids * cap_slot + slot_rank
    pair_tok = jnp.arange(tok_dev * top_k, dtype=jnp.int32) // top_k
    slot_tok = jnp.zeros((n_exp * cap_slot,), jnp.int32).at[slot_idx].set(pair_tok)
    return slot_idx, slot_tok


def solution(mesh):
    n_dev = mesh.shape['ez'] * mesh.shape['ey'] * mesh.shape['ex']

    def local_layer(x_loc, ids_loc, gates_loc, w_g, w_u, w_d):
        tok_dev, hid_dim = x_loc.shape
        top_k = ids_loc.shape[1]
        n_local = w_g.shape[0]
        n_exp = n_local * n_dev
        cap_slot = 2 * tok_dev * top_k // n_exp
        slot_idx, slot_tok = slot_layout(ids_loc, n_exp, cap_slot)
        send_buf = jnp.take(x_loc, slot_tok, axis=0).reshape(n_dev, n_local, cap_slot, hid_dim)
        recv_buf = lax.all_to_all(send_buf, EXPERT_AXES, 0, 0)
        h_gate = jnp.einsum('slch,lhf->slcf', recv_buf, w_g, preferred_element_type=jnp.float32)
        h_up = jnp.einsum('slch,lhf->slcf', recv_buf, w_u, preferred_element_type=jnp.float32)
        act_bf = (jax.nn.silu(h_gate) * h_up).astype(jnp.bfloat16)
        exp_out = jnp.einsum('slcf,lfh->slch', act_bf, w_d, preferred_element_type=jnp.float32).astype(jnp.bfloat16)
        back_buf = lax.all_to_all(exp_out, EXPERT_AXES, 0, 0)
        back_flat = back_buf.reshape(n_exp * cap_slot, hid_dim)
        tok_rows = jnp.take(back_flat, slot_idx, axis=0).reshape(tok_dev, top_k, hid_dim)
        moe_sum = jnp.sum(gates_loc[:, :, None] * tok_rows, axis=1)
        return (x_loc.astype(jnp.float32) + moe_sum).astype(jnp.bfloat16)

    tok_spec = P(TOKEN_AXES, None)
    w_spec = P(EXPERT_AXES, None, None)
    return jax.shard_map(local_layer, mesh=mesh, in_specs=(tok_spec, tok_spec, tok_spec, w_spec, w_spec, w_spec), out_specs=tok_spec, check_vma=False)
```

profile of v0, /device:TPU:0, one launch (start us, length us, event | category | flops | bytes accessed | tf_op | source)
XLA Modules:
  0.0 627.3 jit_solution(2622317267720819154)
XLA Ops:
  0.0 0.0 copy-start
  0.0 1.0 copy.24
  1.0 0.1 eq.26
  1.2 0.1 reshape.85
  1.3 0.7 broadcast_multiply_fusion
  2.0 0.9 fusion.20
  2.9 18.0 %reduce-window.6 = s32[32,32,128]{2,1,0:T(8,128)} reduce-window(s32[32,32,128]{2,1,0:T(8,128)} %fusion.20, s32[]{:T(128)} %constant.52.clone.1), window={size=1x1x128 pad=0_0x0_0x127_0}, to_apply=%region_0.0 | reduce-window | flops 16646144 | bytes 1048580 | tf_op jit(solution)/shard_map/reduce-window
  20.9 1.8 slice_reduce_fusion
  22.7 0.2 reduce-window.9
  22.9 1.2 broadcast_add_fusion
  24.2 0.3 fusion.19
  24.5 0.1 copy.28
  24.7 0.2 mul.41
  24.9 0.0 copy-start.6
  24.9 0.6 copy-done.6
  25.5 15.5 %scatter_custom_fusion = s32[8192]{0:T(1024)S(1)} fusion(s32[4096]{0:T(1024)S(1)} %bitcast.63, s32[4096]{0:T(1024)S(1)} %add_select_fusion, s32[]{:T(128)} %constant.52.clone.1), kind=kCustom, calls=%fused_computation.42 | custom fusion | bytes 32772 | tf_op jit(solution)/shard_map/scatter | solution.py:17
  41.1 35.4 %gather_fusion = bf16[8192,1024]{1,0:T(8,128)(2,1)} fusion(bf16[512,1024]{1,0:T(8,128)(2,1)S(1)} %copy-done.2, s32[8192]{0:T(1024)S(1)} %fusion.21), kind=kCustom, calls=%fused_computation | custom fusion | bytes 33587200 | tf_op jit(solution)/shard_map/jit(_take)/gather | solution.py:31
  76.6 8.5 %broadcast_select_fusion = bf16[16,2,256,1024]{3,2,1,0:T(8,128)(2,1)S(1)} fusion(bf16[16,2,256,1024]{3,2,1,0:T(8,128)(2,1)} %bitcast.59, pred[16,2,256]{2,1,0:T(4,128)(4,1)S(1)} %broadcast_in_dim.32), kind=kLoop, calls=%fused_computation.12 | loop fusion | flops 8388608 | bytes 33562624 | tf_op jit(solution)/shard_map/jit(_take)/select_n | solution.py:31
  85.1 0.0 copy-start.9
  85.1 194.0 %all_to_all.10 = bf16[16,2,256,1024]{3,2,1,0:T(8,128)(2,1)} all-to-all(bf16[16,2,256,1024]{3,2,1,0:T(8,128)(2,1)S(1)} %broadcast_select_fusion), channel_id=1, replica_groups=mesh['ez'=2,'ey'=2,'ex'=4] {'ex','ey','ez'}, dimensions={0} | all-to-all | bytes 33554432 | tf_op jit(solution)/shard_map/all_to_all | solution.py:32
  279.1 15.7 %fusion.4 = f32[2,16,256,512]{3,2,1,0:T(8,128)} fusion(bf16[16,2,256,1024]{3,2,1,0:T(8,128)(2,1)} %all_to_all.10, bf16[2,1024,512]{2,1,0:T(8,128)(2,1)S(1)} %copy-done.9), kind=kOutput, calls=%fused_computation.13 | convolution fusion | flops 8589934592 | bytes 35651584 | tf_op jit(solution)/shard_map/slch,lhf->slcf/dot_general | solution.py:34
  294.8 26.2 %convert_bitcast_fusion = bf16[16,2,256,1024]{3,2,0,1:T(8,128)(2,1)} fusion(f32[2,16,256,512]{3,2,1,0:T(8,128)} %fusion.4, bf16[16,2,256,1024]{3,2,1,0:T(8,128)(2,1)} %all_to_all.10, bf16[2,512,1024]{2,1,0:T(8,128)(2,1)S(1)} %copy-done, bf16[2,1024,512]{2,1,0:T(8,128)(2,1)} %param.9), kind=kOutput, calls=%fused_computation.11 | convolution fusion | flops 17213423616 | bytes 54525952 | tf_op jit(solution)/shard_map/slcf,lfh->slch/dot_general | solution.py:36
  321.0 13.9 %copy.31 = bf16[16,2,256,1024]{3,2,1,0:T(8,128)(2,1)} copy(bf16[16,2,256,1024]{3,2,0,1:T(8,128)(2,1)} %convert_bitcast_fusion) | data formatting | bytes 33554432 | tf_op jit(solution)/shard_map/convert_element_type | solution.py:36
  334.9 4.3 all-to-all-start.1
  339.2 0.2 sub.15
  339.4 0.1 copy.26
  339.5 0.2 copy.27
  339.7 0.1 copy.23
  339.8 248.1 %all-to-all-done.1 = bf16[16,2,256,1024]{3,2,1,0:T(8,128)(2,1)} async-done(((bf16[16,2,256,1024]{3,2,1,0:T(8,128)(2,1)}), bf16[16,2,256,1024]{3,2,1,0:T(8,128)(2,1)}, u32[]{:S(2)}, u32[]{:S(2)}) %all-to-all-start.1) | async-done | bytes 16777248 | tf_op jit(solution)/shard_map/all_to_all | solution.py:37
  587.9 29.0 %gather_fusion.1 = bf16[4096,1024]{1,0:T(8,128)(2,1)} fusion(bf16[8192,1024]{1,0:T(8,128)(2,1)} %bitcast.13, s32[4096]{0:T(1024)S(1)} %broadcast_clamp_fusion), kind=kCustom, calls=%fused_computation.1 | custom fusion | bytes 16793600 | tf_op jit(solution)/shard_map/jit(_take)/gather | solution.py:39
  616.9 9.1 %multiply_reduce_fusion = f32[512,1024]{1,0:T(8,128)S(1)} fusion(bf16[4096,1024]{1,0:T(8,128)(2,1)} %gather_fusion.1, f32[512,8]{1,0:T(8,128)S(1)} %copy.23, pred[512,8]{1,0:T(8,128)(4,1)S(1)} %copy.27), kind=kLoop, calls=%fused_computation.10 | loop fusion | flops 16252928 | bytes 10506240 | tf_op jit(solution)/shard_map/reduce_sum | solution.py:40
  625.9 1.3 add_convert_fusion
  (24 shorter events, 0.1 us)
Async XLA Ops:
  0.0 294.8 %copy-start = (bf16[2,512,1024]{2,1,0:T(8,128)(2,1)S(1)}, bf16[2,512,1024]{2,1,0:T(8,128)(2,1)}, u32[]{:S(2)}) copy-start(bf16[2,512,1024]{2,1,0:T(8,128)(2,1)} %param.11) | copy-start | bytes 6291460
  0.0 41.1 %copy-start.2 = (bf16[512,1024]{1,0:T(8,128)(2,1)S(1)}, bf16[512,1024]{1,0:T(8,128)(2,1)}, u32[]{:S(2)}) copy-start(bf16[512,1024]{1,0:T(8,128)(2,1)} %param.6) | copy-start | bytes 3145732
  24.5 52.0 %copy-start.3 = (s32[4096]{0:T(1024)}, s32[4096]{0:T(1024)S(1)}, u32[]{:S(2)}) copy-start(s32[4096]{0:T(1024)S(1)} %broadcast_add_fusion.1) | copy-start | bytes 49156
  24.9 0.6 copy-start.6
  85.1 194.1 %copy-start.9 = (bf16[2,1024,512]{2,1,0:T(8,128)(2,1)S(1)}, bf16[2,1024,512]{2,1,0:T(8,128)(2,1)}, u32[]{:S(2)}) copy-start(bf16[2,1024,512]{2,1,0:T(8,128)(2,1)} %param.10) | copy-start | bytes 6291460
  334.9 4.3 copy-start.4
  334.9 4.6 copy-start.5
  334.9 4.8 copy-start.8
  334.9 4.9 copy-start.7
  334.9 253.0 %all-to-all-start.1 = ((bf16[16,2,256,1024]{3,2,1,0:T(8,128)(2,1)}), bf16[16,2,256,1024]{3,2,1,0:T(8,128)(2,1)}, u32[]{:S(2)}, u32[]{:S(2)}) async-start(bf16[16,2,256,1024]{3,2,1,0:T(8,128)(2,1)} %copy.31), calls=%async_computation.1 | async-start | bytes 33554432 | tf_op jit(solution)/shard_map/all_to_all | solution.py:37
  587.9 39.4 %copy-start.1 = (bf16[2,512,1024]{2,1,0:T(8,128)(2,1)S(1)}, bf16[2,512,1024]{2,1,0:T(8,128)(2,1)}, u32[]{:S(2)}) copy-start(bf16[2,512,1024]{2,1,0:T(8,128)(2,1)} %param.11) | copy-start | bytes 6291460
where the time goes:
time: 637 us; the launch traced here: 627 us
  waiting for transfers between devices  248 us (39%)
  blocking collectives  194 us (30%)
  local copies, waits for them, and re-layouts  98.4 us (15%)
  matrix products  41.9 us (7%)
  other arithmetic  40.4 us (6%)
    all_to_all x1, waiting for transfers between devices, local_layer(): back_buf = lax.all_to_all(exp_out, EXPERT_AXES, 0, 0)  248 us
    all_to_all x1, blocking collectives, local_layer(): recv_buf = lax.all_to_all(send_buf, EXPERT_AXES, 0, 0)  194 us
    gather x1, local copies, waits for them, and re-layouts, local_layer(): jnp.take(x_loc, slot_tok, axis=0).reshape(n_dev, n_local, cap_slot, hid_dim)  35.4 us
    gather x1, local copies, waits for them, and re-layouts, local_layer(): jnp.take(back_flat, slot_idx, axis=0).reshape(tok_dev, top_k, hid_dim)  29 us
    dot_general x1, matrix products, local_layer(): jnp.einsum('slcf,lfh->slch', act_bf, w_d, preferred_element_type=jnp.floa...  26.2 us
    another operation x3, other arithmetic  19.5 us
    dot_general x1, matrix products, local_layer(): jnp.einsum('slch,lhf->slcf', recv_buf, w_u, preferred_element_type=jnp.fl...  15.7 us
    scatter x1, local copies, waits for them, and re-layouts, slot_layout(): jnp.zeros((n_exp * cap_slot,), jnp.int32).at[slot_idx].set(pair_tok)  15.5 us
  transfers between devices with their start and end apart: 1, of which 1 were waited for; matrix products, arithmetic and copies ran while one was open for 0% of the time, Pallas kernels for 0%

commit v1 on v0

v1 whole, which is shorter than its diff:
```python
import jax
import jax.numpy as jnp
from jax import lax
from jax.experimental import pallas as pl
from jax.experimental.pallas import tpu as pltpu
from jax.sharding import PartitionSpec as P

TOKEN_AXES = ('ez', 'ey', 'ex')
EXPERT_AXES = ('ex', 'ey', 'ez')
MESH = pl.DeviceIdType.MESH

CHIP_MASKS = (0, 2, 4, 8, 6, 10, 12, 14)
Q_OF = {m: q for q, m in enumerate(CHIP_MASKS)}
ORDERS = ((2, 4, 8), (4, 8, 2), (8, 2, 4))
AG_PARTS = ((0, 176), (176, 176), (352, 160))
RS_PARTS = ((0, 176), (176, 168), (344, 168))
HALF = 256


def slot_of(mask):
    return 2 * Q_OF[mask & 14] + (mask & 1)


def peer(mask):
    z, y, e = lax.axis_index('ez'), lax.axis_index('ey'), lax.axis_index('ex')
    x, c = e // 2, e % 2
    z = 1 - z if mask & 8 else z
    y = 1 - y if mask & 4 else y
    x = 1 - x if mask & 2 else x
    c = 1 - c if mask & 1 else c
    return z, y, 2 * x + c


def moe_kernel(x_hbm, g_hbm, w1_hbm, w3_hbm, w2_hbm, y_hbm,
               w1, w3, w2, x_all, g_all, act, acc, rs, dd_in,
               load_sem, g_send, g_recv, ag_send, ag_recv, xd_send, xd_recv,
               rs_send, rs_recv, dd_send, dd_recv, dd_free):
    tok, hid = x_hbm.shape
    partner = peer(1)

    def remote(src, dst, ssem, rsem, mask):
        return pltpu.make_async_remote_copy(src, dst, ssem, rsem, device_id=peer(mask), device_id_type=MESH)

    def expert_place(mask):
        z, y, e = peer(mask)
        return e * 4 + y * 2 + z

    def gate_copy(mask):
        return remote(g_hbm.at[expert_place(mask)], g_all.at[slot_of(mask)], g_send.at[mask], g_recv.at[mask], mask)

    def ag_sources(p):
        d0, d1, d2 = ORDERS[p]
        return ((0, d0), (0, d1), (0, d2), (d0, d1), (d0, d2), (d1, d2), (d0 ^ d1, d2))

    def ag_copy(p, k):
        mask, axis = ag_sources(p)[k]
        r0, n = AG_PARTS[p]
        return remote(x_all.at[slot_of(mask), pl.ds(r0, n)], x_all.at[slot_of(mask ^ axis), pl.ds(r0, n)],
                      ag_send.at[p, k], ag_recv.at[p, k], axis)

    def x_partner_copy(q, p):
        r0, n = (0, tok) if q == 0 else AG_PARTS[p]
        return remote(x_all.at[2 * q, pl.ds(r0, n)], x_all.at[2 * q + 1, pl.ds(r0, n)], xd_send.at[q, p], xd_recv.at[q, p], 1)

    def rs_moves(p):
        e0, e1, e2 = ORDERS[p]
        first = {0: (6, 10), 1: (6, 12), 2: (10, 12)}[p]
        return ((e0, e0), (first[0], e0), (14, e0), (first[1], e0), (e1 ^ e2, e1), (e1, e1), (e2, e2))

    def rs_copy(p, k):
        mask, axis = rs_moves(p)[k]
        r0, n = RS_PARTS[p]
        return remote(acc.at[Q_OF[mask], pl.ds(r0, n)], rs.at[k, pl.ds(r0, n)], rs_send.at[p, k], rs_recv.at[p, k], axis)

    def rs_add(p, k):
        mask, axis = rs_moves(p)[k]
        q = Q_OF[mask ^ axis]
        r0, n = RS_PARTS[p]
        rs_copy(p, k).wait_recv()

        @pl.loop(0, n // 8)
        def _(i):
            rows = pl.ds(pl.multiple_of(r0 + i * 8, 8), 8)
            acc[q, rows, :] = acc[q, rows, :] + rs[k, rows, :]

    def partial_copy(h):
        rows = pl.ds(pl.multiple_of(h * HALF, HALF), HALF)
        return remote(acc.at[8, rows], dd_in.at[h], dd_send.at[h], dd_recv.at[h], 1)

    loads = [pltpu.make_async_copy(s, d, load_sem.at[i]) for i, (s, d) in enumerate((
        (x_hbm, x_all.at[0]), (g_hbm.at[expert_place(0)], g_all.at[0]), (w1_hbm, w1), (w3_hbm, w3), (w2_hbm, w2)))]

    for c in loads:
        c.start()
    barrier = pltpu.get_barrier_semaphore()
    for mask in range(1, 16):
        pl.semaphore_signal(barrier, inc=1, device_id=peer(mask), device_id_type=MESH)
    pl.semaphore_wait(barrier, 15)
    for mask in range(1, 16):
        gate_copy(mask).start()
    loads[0].wait()
    for k in range(3):
        for p in range(3):
            ag_copy(p, k).start()
    x_partner_copy(0, 0).start()
    for c in loads[1:]:
        c.wait()
    for mask in range(1, 16):
        gate_copy(mask).wait_recv()

    def arrived(k, onward):
        for p in range(3):
            ag_copy(p, k).wait_recv()
            for j in onward:
                ag_copy(p, j).start()
            mask, axis = ag_sources(p)[k]
            x_partner_copy(Q_OF[mask ^ axis], p).start()

    def x_ready(q):
        if q == 0:
            x_partner_copy(0, 0).wait_recv()
        else:
            for p in range(3):
                x_partner_copy(q, p).wait_recv()

    def events(q):
        if q == 1:
            arrived(0, (3, 4))
            arrived(1, (5,))
            arrived(2, ())
        if q == 2:
            arrived(3, (6,))
            rs_copy(0, 0).start()
        if q == 3:
            arrived(4, ())
            rs_copy(1, 0).start()
        if q == 4:
            arrived(5, ())
            rs_copy(2, 0).start()
        if q == 5:
            arrived(6, ())
            rs_copy(0, 1).start()
            rs_copy(1, 1).start()
        if q == 6:
            rs_copy(2, 1).start()
        x_ready(q)

    @pl.loop(0, 32)
    def _(step):
        q, turn = step // 4, step % 4
        other = 1 - turn // 2
        h = turn % 2
        for i in range(8):
            @pl.when(step == 4 * i)
            def _(i=i):
                events(i)

        slot = 2 * q + other
        into = q + other * (8 - q)
        r0 = pl.multiple_of(h * HALF, HALF)

        @pl.when(jnp.logical_and(other == 1, q > 0))
        def _():
            partial_copy(h).wait_send()

        gate = g_all[slot].T
        cols = []
        for l in range(2):
            halves = [jnp.where(h == 0, gate[:, 2 * i + l:2 * i + l + 1], gate[:, 4 + 2 * i + l:5 + 2 * i + l]) for i in range(2)]
            cols.append(jnp.concatenate(halves, axis=0))
        for l in range(2):
            for n in range(2):
                cs = slice(n * 256, n * 256 + 256)
                x_in = x_all[slot, pl.ds(r0, HALF), :]
                h1 = jnp.dot(x_in, w1[l, :, cs], preferred_element_type=jnp.float32)
                h3 = jnp.dot(x_in, w3[l, :, cs], preferred_element_type=jnp.float32)
                act[l, :, cs] = (h1 * jax.nn.sigmoid(h1) * h3).astype(jnp.bfloat16)
        for n in range(4):
            cs = slice(n * 256, n * 256 + 256)
            total = None
            for l in range(2):
                o = jnp.dot(act[l], w2[l, :, cs], preferred_element_type=jnp.float32)
                o = o.astype(jnp.bfloat16).astype(jnp.float32)
                term = jnp.where(cols[l] > 0, cols[l] * o, 0.0)
                total = term if total is None else total + term
            acc[into, pl.ds(r0, HALF), cs] = total

        @pl.when(other == 1)
        def _():
            @pl.when(q > 0)
            def _():
                pl.semaphore_wait(dd_free.at[h], 1)
            partial_copy(h).start()

        @pl.when(other == 0)
        def _():
            partial_copy(h).wait_recv()

            @pl.loop(0, HALF // 8)
            def _(i):
                rows = pl.ds(pl.multiple_of(i * 8, 8), 8)
                out = pl.ds(pl.multiple_of(r0 + i * 8, 8), 8)
                acc[q, out, :] = acc[q, out, :] + dd_in[h, rows, :]

            @pl.when(q < 7)
            def _():
                pl.semaphore_signal(dd_free.at[h], inc=1, device_id=partner, device_id_type=MESH)

    for p in range(3):
        rs_copy(p, 2).start()
    for p in range(3):
        rs_copy(p, 3).start()
    for k in (0, 1):
        for p in range(3):
            rs_add(p, k)
    for p in range(3):
        rs_add(p, 2)
        rs_copy(p, 4).start()
    for p in range(3):
        rs_add(p, 3)
        rs_copy(p, 5).start()
    for p in range(3):
        rs_add(p, 4)
        rs_copy(p, 6).start()
    for p in range(3):
        rs_add(p, 5)
    for p in range(3):
        rs_copy(p, 6).wait_recv()

    @pl.loop(0, tok // 16)
    def _(i):
        rows = pl.ds(pl.multiple_of(i * 16, 16), 16)
        x_all[1, rows, :] = (x_all[0, rows, :].astype(jnp.float32) + (acc[0, rows, :] + rs[6, rows, :])).astype(jnp.bfloat16)

    store = pltpu.make_async_copy(x_all.at[1], y_hbm, load_sem.at[0])
    store.start()
    for mask in range(1, 16):
        gate_copy(mask).wait_send()
    for p in range(3):
        for k in range(7):
            ag_copy(p, k).wait_send()
            rs_copy(p, k).wait_send()
    x_partner_copy(0, 0).wait_send()
    for q in range(1, 8):
        for p in range(3):
            x_partner_copy(q, p).wait_send()
    for h in range(2):
        partial_copy(h).wait_send()
    store.wait()


def solution(mesh):
    n_dev = mesh.shape['ez'] * mesh.shape['ey'] * mesh.shape['ex']

    def local_layer(x_loc, ids_loc, gates_loc, w_g, w_u, w_d):
        tok, hid = x_loc.shape
        n_local, _, ffn = w_g.shape
        n_exp = n_local * n_dev
        hit = ids_loc[:, :, None] == jnp.arange(n_exp)[None, None, :]
        dense_g = jnp.sum(jnp.where(hit, gates_loc[:, :, None], 0.0), axis=1)
        tiles = dense_g.T.reshape(n_dev, n_local, 4, 128).transpose(0, 2, 1, 3).reshape(n_dev, 8, 128)
        hbm = pl.BlockSpec(memory_space=pl.ANY)
        dma = pltpu.SemaphoreType.DMA
        return pl.pallas_call(
            moe_kernel,
            out_shape=jax.ShapeDtypeStruct((tok, hid), jnp.bfloat16),
            in_specs=[hbm] * 5,
            out_specs=hbm,
            scratch_shapes=[
                pltpu.VMEM((n_local, hid, ffn), jnp.bfloat16),
                pltpu.VMEM((n_local, hid, ffn), jnp.bfloat16),
                pltpu.VMEM((n_local, ffn, hid), jnp.bfloat16),
                pltpu.VMEM((n_dev, tok, hid), jnp.bfloat16),
                pltpu.VMEM((n_dev, 8, 128), jnp.float32),
                pltpu.VMEM((n_local, HALF, ffn), jnp.bfloat16),
                pltpu.VMEM((9, tok, hid), jnp.float32),
                pltpu.VMEM((7, tok, hid), jnp.float32),
                pltpu.VMEM((2, HALF, hid), jnp.float32),
                dma((5,)), dma((16,)), dma((16,)), dma((3, 7)), dma((3, 7)), dma((8, 3)), dma((8, 3)),
                dma((3, 7)), dma((3, 7)), dma((2,)), dma((2,)), pltpu.SemaphoreType.REGULAR((2,)),
            ],
            compiler_params=pltpu.CompilerParams(collective_id=0, has_side_effects=True, vmem_limit_bytes=66_000_000),
            name='moe_kernel',
        )(x_loc, tiles, w_g, w_u, w_d)

    tok_spec = P(TOKEN_AXES, None)
    w_spec = P(EXPERT_AXES, None, None)
    return jax.shard_map(local_layer, mesh=mesh, in_specs=(tok_spec, tok_spec, tok_spec, w_spec, w_spec, w_spec), out_specs=tok_spec, check_vma=False)
```

time: 637 us -> 182 us (0.29); the launches traced: 627 us -> 182 us
  waiting for transfers between devices: 248 us -> 0 us
  blocking collectives: 194 us -> 0 us
  Pallas kernels: 0 us -> 178 us
  local copies, waits for them, and re-layouts: 98.4 us -> 2.95 us
  matrix products: 41.9 us -> 0 us
  other arithmetic: 40.4 us -> 0.8 us
    all_to_all x1 -> x0, waiting for transfers between devices: 248 us -> none  [local_layer(): back_buf = lax.all_to_all(exp_out, EXPERT_AXES, 0, 0)]
    all_to_all x1 -> x0, blocking collectives: 194 us -> none  [local_layer(): recv_buf = lax.all_to_all(send_buf, EXPERT_AXES, 0, 0)]
    pallas_call x0 -> x1, Pallas kernels: none -> 178 us  [local_layer(): pl.pallas_call(moe_kernel, out_shape=jax.ShapeDtypeStruct((tok, hid), jnp...]
    gather x2 -> x0, local copies, waits for them, and re-layouts: 64.4 us -> none  [the longest x1 35.4 us: local_layer(): jnp.take(x_loc, slot_tok, axis=0).reshape(n_dev, n_local, cap_slot, hid_dim)]
    dot_general x2 -> x0, matrix products: 41.9 us -> none  [the longest x1 26.2 us: local_layer(): jnp.einsum('slcf,lfh->slch', act_bf, w_d, preferred_element_type=jnp.floa...]
    another operation x3 -> x0, other arithmetic: 19.5 us -> none
    scatter x1 -> x0, local copies, waits for them, and re-layouts: 15.5 us -> none  [slot_layout(): jnp.zeros((n_exp * cap_slot,), jnp.int32).at[slot_idx].set(pair_tok)]
    convert_element_type x1 -> x0, local copies, waits for them, and re-layouts: 13.9 us -> none  [local_layer(): jnp.einsum('slcf,lfh->slch', act_bf, w_d, preferred_element_type=jnp.floa...]
  transfers between devices with their start and end apart: 1 -> 0, of which waited for: 1 -> 0; matrix products, arithmetic and copies ran while one was open for 0% -> 0% of each run, Pallas kernels for 0% -> 0%
where the time goes in v1:
time: 182 us
  Pallas kernels  178 us (98%)
  local copies, waits for them, and re-layouts  2.95 us (2%)
    pallas_call x1, Pallas kernels, local_layer(): pl.pallas_call(moe_kernel, out_shape=jax.ShapeDtypeStruct((tok, hid), jnp...  178 us

profile of v1, /device:TPU:0, one launch (start us, length us, event | category | flops | bytes accessed | tf_op | source)
XLA Modules:
  0.0 181.8 jit_solution(10158979341516104865)
XLA Ops:
  0.0 0.8 select_reduce_fusion
  0.8 0.7 copy.12
  1.5 178.1 %moe_kernel.1 = bf16[512,1024]{1,0:T(8,128)(2,1)} custom-call(bf16[512,1024]{1,0:T(8,128)(2,1)} %x_hbm.1, f32[16,8,128]{2,1,0:T(8,128)} %bitcast.3, bf16[2,1024,512]{2,1,0:T(8,128)(2,1)} %w1_hbm.1, bf16[2,1024,512]{2,1,0:T(8,128)(2,1)} %w3_hbm.1, bf16[2,512,1024]{2,1,0:T(8,128)(2,1)} %w2_hbm.1), custom_call_target="tpu_custom_call" | custom-call | tf_op jit(solution)/shard_map/moe_kernel/pallas_call | solution.py:264
  179.6 2.3 %copy.14 = bf16[512,1024]{1,0:T(8,128)(2,1)} copy(bf16[512,1024]{1,0:T(8,128)(2,1)} %moe_kernel.1) | data formatting | bytes 2097152
  (1 shorter events, 0.0 us)

commit v2 on v0

v2 whole, which is shorter than its diff:
```python
import jax
import jax.numpy as jnp
from jax import lax
from jax.experimental import pallas as pl
from jax.experimental.pallas import tpu as pltpu
from jax.sharding import PartitionSpec as P

TOKEN_AXES = ('ez', 'ey', 'ex')
EXPERT_AXES = ('ex', 'ey', 'ez')
MESH = pl.DeviceIdType.MESH

ORDERS = ((2, 4, 8), (4, 8, 2), (8, 2, 4))
MASKS = tuple((0, a, b, c, a ^ b, a ^ c, b ^ c, 14) for a, b, c in ORDERS)
COUNTS = (176, 176, 160)
STARTS = (0, 176, 352)
GATHER = ((0, 0), (0, 1), (0, 2), (1, 1), (1, 2), (2, 2), (4, 2))
ONWARD = {0: (3, 4), 1: (5,), 2: (), 3: (6,), 4: (), 5: (), 6: ()}
REDUCE = ((1, 0, 0), (4, 2, 0), (7, 6, 0), (5, 3, 0), (6, 3, 1), (2, 0, 1), (3, 0, 2))
BITS = (2, 4, 8, 1)
PATHS = {m: [b for b in BITS if m & b] for m in range(16)}
TILE_MOVES = (
    [(0, m) for m in range(1, 16)],
    [(1, m) for m in range(16) if len(PATHS[m]) > 1],
    [(2, m) for m in (7, 11, 13)],
    [(2, m) for m in (14, 15)],
    [(3, 15)],
)
HALF = 256
QUARTER = 128


def peer(mask):
    z, y, e = lax.axis_index('ez'), lax.axis_index('ey'), lax.axis_index('ex')
    x, c = e // 2, e % 2
    z = 1 - z if mask & 8 else z
    y = 1 - y if mask & 4 else y
    x = 1 - x if mask & 2 else x
    c = 1 - c if mask & 1 else c
    return z, y, 2 * x + c


def moe_kernel(x_hbm, ids_hbm, gates_hbm, w1_hbm, w3_hbm, w2_hbm, sum_hbm, last_hbm,
               w1, w3, w2, ids, gates, x_all, tiles, merged, act, acc, rs, dd_out, dd_in,
               load_sem, gt_send, gt_recv, ag_send, ag_recv, xd_send, xd_recv,
               rs_send, rs_recv, dd_send, dd_recv, dd_free):
    tok = x_hbm.shape[0]

    def remote(src, dst, ssem, rsem, mask):
        return pltpu.make_async_remote_copy(src, dst, ssem, rsem, device_id=peer(mask), device_id_type=MESH)

    def drain(ref, sem):
        pltpu.make_async_copy(ref, ref, sem).wait()

    def part(p):
        return pl.ds(STARTS[p], COUNTS[p])

    def gather_start(k):
        w, a = GATHER[k]
        for p in range(3):
            remote(x_all.at[2 * w, part(p)], x_all.at[2 * (k + 1), part(p)], ag_send, ag_recv.at[k], ORDERS[p][a]).start()

    def gather_wait(k):
        drain(x_all.at[2 * (k + 1)], ag_recv.at[k])

    def pair_copy(w):
        return remote(x_all.at[2 * w], x_all.at[2 * w + 1], xd_send, xd_recv.at[w], 1)

    def reduce_start(k):
        w, _, a = REDUCE[k]
        for p in range(3):
            dst = last_hbm.at[part(p)] if k == 6 else rs.at[k, part(p)]
            remote(acc.at[w, part(p)], dst, rs_send, rs_recv.at[k], ORDERS[p][a]).start()

    def reduce_wait(k):
        drain(acc.at[0], rs_recv.at[k])

    def partial_copy(s):
        return remote(dd_out.at[s], dd_in.at[s], dd_send.at[s], dd_recv.at[s], 1)

    def tiles_start(g):
        for hop, m in TILE_MOVES[g]:
            remote(tiles.at[hop, m], tiles.at[hop + 1, m], gt_send, gt_recv.at[g], PATHS[m][hop]).start()

    def tiles_wait(g):
        drain(tiles.at[0, pl.ds(0, len(TILE_MOVES[g]))], gt_recv.at[g])

    x_load = pltpu.make_async_copy(x_hbm, x_all.at[0], load_sem.at[0])
    loads = [pltpu.make_async_copy(s, d, load_sem.at[1 + i]) for i, (s, d) in enumerate((
        (ids_hbm, ids), (gates_hbm, gates), (w1_hbm, w1), (w3_hbm, w3), (w2_hbm, w2)))]

    barrier = pltpu.get_barrier_semaphore()
    for mask in BITS:
        pl.semaphore_signal(barrier, inc=1, device_id=peer(mask), device_id_type=MESH)
    x_load.start()
    for c in loads:
        c.start()
    for c in loads[:2]:
        c.wait()
    for m in range(16):
        z, y, e = peer(m)
        for l in range(2):
            hit = ids[...] == 2 * (e * 4 + y * 2 + z) + l
            row = jnp.sum(jnp.where(hit, gates[...], 0.0), axis=0, keepdims=True)
            for q in range(4):
                tiles[0, m, pl.ds(2 * q + l, 1), :] = row[:, q * QUARTER:(q + 1) * QUARTER]
    x_load.wait()
    pl.semaphore_wait(barrier, 4)
    tiles_start(0)
    gather_start(0)
    pair_copy(0).start()
    tiles_wait(0)
    tiles_start(1)
    gather_start(1)
    gather_start(2)
    for c in loads[2:]:
        c.wait()

    def merge_tiles(w):
        token = lax.broadcasted_iota(jnp.int32, (8, QUARTER), 0) // 2 * QUARTER + lax.broadcasted_iota(jnp.int32, (8, QUARTER), 1)
        for side in range(2):
            t = [tiles[len(PATHS[MASKS[p][w] | side]), MASKS[p][w] | side] for p in range(3)]
            merged[2 * w + side] = jnp.where(token < STARTS[1], t[0], jnp.where(token < STARTS[2], t[1], t[2]))

    def before(j):
        if j % 2 == 1 and j < 14:
            w = (j + 1) // 2
            gather_wait(w - 1)
            for k in ONWARD[w - 1]:
                gather_start(k)
            pair_copy(w).start()
        if j == 1:
            tiles_wait(1)
            tiles_start(2)
            tiles_start(3)
        if j == 8:
            tiles_wait(2)
        if j == 13:
            tiles_wait(3)
            tiles_start(4)
        if j == 14:
            tiles_wait(4)
        if j % 2 == 0 and j < 16:
            merge_tiles(j // 2)
            pair_copy(j // 2).wait_recv()

    def after(j):
        if j == 7:
            reduce_start(0)
        if j == 10:
            reduce_start(1)

    def up(slot, rows):
        for l in range(2):
            for n in range(2):
                cs = slice(n * 256, n * 256 + 256)
                x_in = x_all[slot, rows, :]
                h1 = jnp.dot(x_in, w1[l, :, cs], preferred_element_type=jnp.float32)
                h3 = jnp.dot(x_in, w3[l, :, cs], preferred_element_type=jnp.float32)
                act[l, :, cs] = (h1 * jax.nn.sigmoid(h1) * h3).astype(jnp.bfloat16)

    def down(slot, h, store):
        columns = merged[slot].T
        gate = []
        for l in range(2):
            halves = [jnp.where(h == 0, columns[:, 2 * i + l:2 * i + l + 1], columns[:, 4 + 2 * i + l:5 + 2 * i + l]) for i in range(2)]
            gate.append(jnp.concatenate(halves, axis=0))
        for n in range(4):
            cs = slice(n * 256, n * 256 + 256)
            total = None
            for l in range(2):
                o = jnp.dot(act[l], w2[l, :, cs], preferred_element_type=jnp.float32)
                o = o.astype(jnp.bfloat16).astype(jnp.float32)
                term = jnp.where(gate[l] > 0, gate[l] * o, 0.0)
                total = term if total is None else total + term
            store(cs, total)

    @pl.loop(0, 17)
    def _(i):
        for j in range(16):
            @pl.when(i == j)
            def _(j=j):
                before(j)

        @pl.when(i < 16)
        def _():
            w, h = i // 2, i % 2
            rows = pl.ds(pl.multiple_of(h * HALF, HALF), HALF)

            @pl.when(i >= 2)
            def _():
                partial_copy(h).wait_send()

            up(2 * w + 1, rows)

            def store(cs, total):
                dd_out[h, :, cs] = total

            down(2 * w + 1, h, store)

            @pl.when(i >= 2)
            def _():
                pl.semaphore_wait(dd_free.at[h], 1)

            partial_copy(h).start()

        @pl.when(i > 0)
        def _():
            w, h = (i - 1) // 2, (i - 1) % 2
            rows = pl.ds(pl.multiple_of(h * HALF, HALF), HALF)
            up(2 * w, rows)
            partial_copy(h).wait_recv()

            def store(cs, total):
                acc[w, rows, cs] = total + dd_in[h, :, cs]

            down(2 * w, h, store)

            @pl.when(i < 15)
            def _():
                pl.semaphore_signal(dd_free.at[h], inc=1, device_id=peer(1), device_id_type=MESH)

        for j in (7, 10):
            @pl.when(i == j)
            def _(j=j):
                after(j)

    reduce_start(2)
    reduce_start(3)

    def add(k):
        _, w, _ = REDUCE[k]
        reduce_wait(k)

        @pl.loop(0, tok // 16)
        def _(i):
            rows = pl.ds(pl.multiple_of(i * 16, 16), 16)
            got = acc[w, rows, :] + rs[k, rows, :]
            if k == 5:
                got = got + x_all[0, rows, :].astype(jnp.float32)
            acc[w, rows, :] = got

    add(0)
    add(1)
    add(2)
    reduce_start(4)
    reduce_start(5)
    add(3)
    add(4)
    reduce_start(6)
    add(5)
    store = pltpu.make_async_copy(acc.at[0], sum_hbm, load_sem.at[0])
    store.start()

    drain(tiles.at[pl.ds(0, 2)], gt_send)
    drain(x_all.at[pl.ds(0, 7)], ag_send)
    drain(x_all.at[pl.ds(0, 8)], xd_send)
    for h in range(2):
        partial_copy(h).wait_send()
    store.wait()
    drain(acc.at[pl.ds(0, 7)], rs_send)
    reduce_wait(6)


def final_kernel(a_hbm, b_hbm, y_hbm, a, b, y, in_sem, out_sem):
    n = in_sem.shape[0]
    rows = a.shape[0] // n
    loads, stores = [], []
    for c in range(n):
        part = pl.ds(c * rows, rows)
        loads.append([pltpu.make_async_copy(s.at[part], d.at[part], in_sem.at[c, i]) for i, (s, d) in enumerate(((a_hbm, a), (b_hbm, b)))])
        stores.append(pltpu.make_async_copy(y.at[part], y_hbm.at[part], out_sem.at[c]))
        for copy in loads[c]:
            copy.start()
    for c in range(n):
        for copy in loads[c]:
            copy.wait()

        @pl.loop(0, rows // 16)
        def _(i):
            at = pl.ds(pl.multiple_of(c * rows + i * 16, 16), 16)
            y[at, :] = (a[at, :] + b[at, :]).astype(y.dtype)

        stores[c].start()
    for copy in stores:
        copy.wait()


def solution(mesh):
    n_dev = mesh.shape['ez'] * mesh.shape['ey'] * mesh.shape['ex']

    def local_layer(x_loc, ids_loc, gates_loc, w_g, w_u, w_d):
        tok, hid = x_loc.shape
        top_k = ids_loc.shape[1]
        n_local, _, ffn = w_g.shape
        hbm = pl.BlockSpec(memory_space=pl.ANY)
        dma = pltpu.SemaphoreType.DMA
        f32, bf16 = jnp.float32, jnp.bfloat16
        total, last = pl.pallas_call(
            moe_kernel,
            out_shape=[jax.ShapeDtypeStruct((tok, hid), f32)] * 2,
            in_specs=[hbm] * 6,
            out_specs=[hbm] * 2,
            scratch_shapes=[
                pltpu.VMEM((n_local, hid, ffn), bf16),
                pltpu.VMEM((n_local, hid, ffn), bf16),
                pltpu.VMEM((n_local, ffn, hid), bf16),
                pltpu.VMEM((top_k, tok), jnp.int32),
                pltpu.VMEM((top_k, tok), f32),
                pltpu.VMEM((n_dev, tok, hid), bf16),
                pltpu.VMEM((5, n_dev, 8, QUARTER), f32),
                pltpu.VMEM((n_dev, 8, QUARTER), f32),
                pltpu.VMEM((n_local, HALF, ffn), bf16),
                pltpu.VMEM((8, tok, hid), f32),
                pltpu.VMEM((6, tok, hid), f32),
                pltpu.VMEM((2, HALF, hid), f32),
                pltpu.VMEM((2, HALF, hid), f32),
                dma((6,)), dma, dma((5,)), dma, dma((7,)), dma, dma((8,)),
                dma, dma((7,)), dma((2,)), dma((2,)), pltpu.SemaphoreType.REGULAR((2,)),
            ],
            compiler_params=pltpu.CompilerParams(collective_id=0, has_side_effects=True, vmem_limit_bytes=66_000_000),
            name='moe_kernel',
        )(x_loc, ids_loc.T, gates_loc.T, w_g, w_u, w_d)
        return pl.pallas_call(
            final_kernel,
            out_shape=jax.ShapeDtypeStruct((tok, hid), bf16),
            in_specs=[hbm] * 2,
            out_specs=hbm,
            scratch_shapes=[pltpu.VMEM((tok, hid), f32), pltpu.VMEM((tok, hid), f32), pltpu.VMEM((tok, hid), bf16), dma((4, 2)), dma((4,))],
            name='final_kernel',
        )(total, last)

    tok_spec = P(TOKEN_AXES, None)
    w_spec = P(EXPERT_AXES, None, None)
    return jax.shard_map(local_layer, mesh=mesh, in_specs=(tok_spec, tok_spec, tok_spec, w_spec, w_spec, w_spec), out_specs=tok_spec, check_vma=False)
```

time: 637 us -> 167 us (0.26); the launches traced: 627 us -> 167 us
  waiting for transfers between devices: 248 us -> 0 us
  blocking collectives: 194 us -> 0 us
  Pallas kernels: 0 us -> 167 us
  local copies, waits for them, and re-layouts: 98.4 us -> 0 us
  matrix products: 41.9 us -> 0 us
  other arithmetic: 40.4 us -> 0 us
    all_to_all x1 -> x0, waiting for transfers between devices: 248 us -> none  [local_layer(): back_buf = lax.all_to_all(exp_out, EXPERT_AXES, 0, 0)]
    all_to_all x1 -> x0, blocking collectives: 194 us -> none  [local_layer(): recv_buf = lax.all_to_all(send_buf, EXPERT_AXES, 0, 0)]
    pallas_call x0 -> x2, Pallas kernels: none -> 167 us  [the longest x1 164 us: local_layer(): pl.pallas_call(moe_kernel, out_shape=[jax.ShapeDtypeStruct((tok, hid), f3...]
    gather x2 -> x0, local copies, waits for them, and re-layouts: 64.4 us -> none  [the longest x1 35.4 us: local_layer(): jnp.take(x_loc, slot_tok, axis=0).reshape(n_dev, n_local, cap_slot, hid_dim)]
    dot_general x2 -> x0, matrix products: 41.9 us -> none  [the longest x1 26.2 us: local_layer(): jnp.einsum('slcf,lfh->slch', act_bf, w_d, preferred_element_type=jnp.floa...]
    another operation x3 -> x0, other arithmetic: 19.5 us -> none
    scatter x1 -> x0, local copies, waits for them, and re-layouts: 15.5 us -> none  [slot_layout(): jnp.zeros((n_exp * cap_slot,), jnp.int32).at[slot_idx].set(pair_tok)]
    convert_element_type x1 -> x0, local copies, waits for them, and re-layouts: 13.9 us -> none  [local_layer(): jnp.einsum('slcf,lfh->slch', act_bf, w_d, preferred_element_type=jnp.floa...]
  transfers between devices with their start and end apart: 1 -> 0, of which waited for: 1 -> 0; matrix products, arithmetic and copies ran while one was open for 0% -> 0% of each run, Pallas kernels for 0% -> 0%
where the time goes in v2:
time: 167 us
  Pallas kernels  167 us (100%)
    pallas_call x1, Pallas kernels, local_layer(): pl.pallas_call(moe_kernel, out_shape=[jax.ShapeDtypeStruct((tok, hid), f3...  164 us

profile of v2, /device:TPU:0, one launch (start us, length us, event | category | flops | bytes accessed | tf_op | source)
XLA Modules:
  0.0 167.4 jit_solution(5498984769284424184)
XLA Ops:
  0.0 164.3 %moe_kernel.1 = (f32[512,1024]{1,0:T(8,128)}, f32[512,1024]{1,0:T(8,128)}) custom-call(bf16[512,1024]{1,0:T(8,128)(2,1)} %x_hbm.1, s32[8,512]{1,0:T(8,128)} %bitcast.2, f32[8,512]{1,0:T(8,128)} %bitcast.3, bf16[2,1024,512]{2,1,0:T(8,128)(2,1)} %w1_hbm.1, bf16[2,1024,512]{2,1,0:T(8,128)(2,1)} %w3_hbm.1, bf16[2,512,1024]{2,1,0:T(8,128)(2,1)} %w2_hbm.1), custom_call_target="tpu_custom_call" | custom-call | tf_op jit(solution)/shard_map/moe_kernel/pallas_call | solution.py:298
  164.3 3.0 %final_kernel.1 = bf16[512,1024]{1,0:T(8,128)(2,1)} custom-call(f32[512,1024]{1,0:T(8,128)} %get-tuple-element.7.a_hbm, f32[512,1024]{1,0:T(8,128)} %get-tuple-element.8.b_hbm), custom_call_target="tpu_custom_call" | custom-call | tf_op jit(solution)/shard_map/final_kernel/pallas_call | solution.py:323

commit v3 on v2

--- a/solution.py
+++ b/solution.py
@@ -9,13 +9,32 @@
 EXPERT_AXES = ('ex', 'ey', 'ez')
 MESH = pl.DeviceIdType.MESH
 
-ORDERS = ((2, 4, 8), (4, 8, 2), (8, 2, 4))
-MASKS = tuple((0, a, b, c, a ^ b, a ^ c, b ^ c, 14) for a, b, c in ORDERS)
-COUNTS = (176, 176, 160)
-STARTS = (0, 176, 352)
+PARTS = (
+    (0, 160, (2, 4, 8), (2, 4, 8)),
+    (160, 160, (4, 8, 2), (4, 8, 2)),
+    (320, 160, (8, 2, 4), (8, 2, 4)),
+    (480, 16, (2, 4, 8), (2, 8, 4)),
+    (496, 16, (2, 4, 8), (4, 2, 8)),
+)
 GATHER = ((0, 0), (0, 1), (0, 2), (1, 1), (1, 2), (2, 2), (4, 2))
 ONWARD = {0: (3, 4), 1: (5,), 2: (), 3: (6,), 4: (), 5: (), 6: ()}
-REDUCE = ((1, 0, 0), (4, 2, 0), (7, 6, 0), (5, 3, 0), (6, 3, 1), (2, 0, 1), (3, 0, 2))
+
+
+def masks(part):
+    a, b, c = part[2]
+    return 0, a, b, c, a ^ b, a ^ c, b ^ c, 14
+
+
+def reduce_move(part, k):
+    a, b, c = part[3]
+    mask, axis = ((a, a), (a ^ b, a), (14, a), (a ^ c, a), (b ^ c, b), (b, b), (c, c))[k]
+    return masks(part).index(mask), masks(part).index(mask ^ axis), axis
+
+
+FIRST = [(r, 128, part) for part in PARTS[:3] for r in part[:1]]
+SECOND = [(part[0] + 128, 32, part) for part in PARTS[:3]] + [(part[0], part[1], part) for part in PARTS[3:]]
+SECOND_AT = (0, 32, 64, 96, 112)
+SECOND_ROWS = 128
 BITS = (2, 4, 8, 1)
 PATHS = {m: [b for b in BITS if m & b] for m in range(16)}
 TILE_MOVES = (
@@ -39,7 +58,7 @@
     return z, y, 2 * x + c
 
 
-def moe_kernel(x_hbm, ids_hbm, gates_hbm, w1_hbm, w3_hbm, w2_hbm, sum_hbm, last_hbm,
+def moe_kernel(x_hbm, ids_hbm, gates_hbm, w1_hbm, w3_hbm, w2_hbm, y_hbm, sum_hbm, last_hbm,
                w1, w3, w2, ids, gates, x_all, tiles, merged, act, acc, rs, dd_out, dd_in,
                load_sem, gt_send, gt_recv, ag_send, ag_recv, xd_send, xd_recv,
                rs_send, rs_recv, dd_send, dd_recv, dd_free):
@@ -51,13 +70,11 @@
     def drain(ref, sem):
         pltpu.make_async_copy(ref, ref, sem).wait()
 
-    def part(p):
-        return pl.ds(STARTS[p], COUNTS[p])
-
     def gather_start(k):
         w, a = GATHER[k]
-        for p in range(3):
-            remote(x_all.at[2 * w, part(p)], x_all.at[2 * (k + 1), part(p)], ag_send, ag_recv.at[k], ORDERS[p][a]).start()
+        for part in PARTS:
+            rows = pl.ds(part[0], part[1])
+            remote(x_all.at[2 * w, rows], x_all.at[2 * (k + 1), rows], ag_send, ag_recv.at[k], part[2][a]).start()
 
     def gather_wait(k):
         drain(x_all.at[2 * (k + 1)], ag_recv.at[k])
@@ -65,14 +82,23 @@
     def pair_copy(w):
         return remote(x_all.at[2 * w], x_all.at[2 * w + 1], xd_send, xd_recv.at[w], 1)
 
-    def reduce_start(k):
-        w, _, a = REDUCE[k]
-        for p in range(3):
-            dst = last_hbm.at[part(p)] if k == 6 else rs.at[k, part(p)]
-            remote(acc.at[w, part(p)], dst, rs_send, rs_recv.at[k], ORDERS[p][a]).start()
+    def reduce_start(k, parts=PARTS):
+        for part in parts:
+            w, _, axis = reduce_move(part, k)
+            rows = pl.ds(part[0], part[1])
+            remote(acc.at[w, rows], rs.at[k, rows], rs_send, rs_recv.at[k], axis).start()
+
+    def reduce_last_start():
+        for r, n, part in FIRST:
+            w, _, axis = reduce_move(part, 6)
+            remote(acc.at[w, pl.ds(r, n)], rs.at[6, pl.ds(r, n)], rs_send, rs_recv.at[6], axis).start()
+        for at, (r, n, part) in zip(SECOND_AT, SECOND):
+            w, _, axis = reduce_move(part, 6)
+            remote(acc.at[w, pl.ds(r, n)], last_hbm.at[pl.ds(at, n)], rs_send, rs_recv.at[7], axis).start()
 
     def reduce_wait(k):
-        drain(acc.at[0], rs_recv.at[k])
+        rows = tok if k < 6 else SECOND_ROWS if k == 7 else tok - SECOND_ROWS
+        drain(acc.at[0, pl.ds(0, rows)], rs_recv.at[k])
 
     def partial_copy(s):
         return remote(dd_out.at[s], dd_in.at[s], dd_send.at[s], dd_recv.at[s], 1)
@@ -118,8 +144,12 @@
     def merge_tiles(w):
         token = lax.broadcasted_iota(jnp.int32, (8, QUARTER), 0) // 2 * QUARTER + lax.broadcasted_iota(jnp.int32, (8, QUARTER), 1)
         for side in range(2):
-            t = [tiles[len(PATHS[MASKS[p][w] | side]), MASKS[p][w] | side] for p in range(3)]
-            merged[2 * w + side] = jnp.where(token < STARTS[1], t[0], jnp.where(token < STARTS[2], t[1], t[2]))
+            tile = None
+            for part in PARTS:
+                m = masks(part)[w] | side
+                mine = tiles[len(PATHS[m]), m]
+                tile = mine if tile is None else jnp.where(token < part[0], tile, mine)
+            merged[2 * w + side] = tile
 
     def before(j):
         if j % 2 == 1 and j < 14:
@@ -147,7 +177,7 @@
         if j == 7:
             reduce_start(0)
         if j == 10:
-            reduce_start(1)
+            reduce_start(1, PARTS[:3])
 
     def up(slot, rows):
         for l in range(2):
@@ -224,20 +254,27 @@
             def _(j=j):
                 after(j)
 
+    reduce_start(1, PARTS[3:])
     reduce_start(2)
     reduce_start(3)
 
+    def sum_rows(first, n, fn):
+        @pl.loop(0, n // 16)
+        def _(i):
+            fn(pl.ds(pl.multiple_of(first + i * 16, 16), 16))
+
     def add(k):
-        _, w, _ = REDUCE[k]
         reduce_wait(k)
-
-        @pl.loop(0, tok // 16)
-        def _(i):
-            rows = pl.ds(pl.multiple_of(i * 16, 16), 16)
-            got = acc[w, rows, :] + rs[k, rows, :]
-            if k == 5:
-                got = got + x_all[0, rows, :].astype(jnp.float32)
-            acc[w, rows, :] = got
+        for first, n, part in ((0, 480, PARTS[0]), (480, 16, PARTS[3]), (496, 16, PARTS[4])):
+            w = reduce_move(part, k)[1]
+
+            def one(rows, w=w):
+                got = acc[w, rows, :] + rs[k, rows, :]
+                if k == 5:
+                    got = got + x_all[0, rows, :].astype(jnp.float32)
+                acc[w, rows, :] = got
+
+            sum_rows(first, n, one)
 
     add(0)
     add(1)
@@ -246,43 +283,52 @@
     reduce_start(5)
     add(3)
     add(4)
-    reduce_start(6)
+    reduce_last_start()
     add(5)
-    store = pltpu.make_async_copy(acc.at[0], sum_hbm, load_sem.at[0])
-    store.start()
+    stores = [pltpu.make_async_copy(acc.at[0, pl.ds(r, n)], sum_hbm.at[pl.ds(at, n)], load_sem.at[i])
+              for i, (at, (r, n, _)) in enumerate(zip(SECOND_AT, SECOND))]
+    for c in stores:
+        c.start()
 
     drain(tiles.at[pl.ds(0, 2)], gt_send)
     drain(x_all.at[pl.ds(0, 7)], ag_send)
     drain(x_all.at[pl.ds(0, 8)], xd_send)
     for h in range(2):
         partial_copy(h).wait_send()
-    store.wait()
+    for c in stores:
+        c.wait()
+
+    reduce_wait(6)
+    stores = []
+    for i, (r, n, _) in enumerate(FIRST):
+        def one(rows):
+            x_all[1, rows, :] = (acc[0, rows, :] + rs[6, rows, :]).astype(x_all.dtype)
+
+        sum_rows(r, n, one)
+        stores.append(pltpu.make_async_copy(x_all.at[1, pl.ds(r, n)], y_hbm.at[pl.ds(r, n)], load_sem.at[i]))
+        stores[i].start()
+    for c in stores:
+        c.wait()
     drain(acc.at[pl.ds(0, 7)], rs_send)
-    reduce_wait(6)
-
-
-def final_kernel(a_hbm, b_hbm, y_hbm, a, b, y, in_sem, out_sem):
-    n = in_sem.shape[0]
-    rows = a.shape[0] // n
-    loads, stores = [], []
-    for c in range(n):
-        part = pl.ds(c * rows, rows)
-        loads.append([pltpu.make_async_copy(s.at[part], d.at[part], in_sem.at[c, i]) for i, (s, d) in enumerate(((a_hbm, a), (b_hbm, b)))])
-        stores.append(pltpu.make_async_copy(y.at[part], y_hbm.at[part], out_sem.at[c]))
-        for copy in loads[c]:
-            copy.start()
-    for c in range(n):
-        for copy in loads[c]:
-            copy.wait()
-
-        @pl.loop(0, rows // 16)
-        def _(i):
-            at = pl.ds(pl.multiple_of(c * rows + i * 16, 16), 16)
-            y[at, :] = (a[at, :] + b[at, :]).astype(y.dtype)
-
-        stores[c].start()
-    for copy in stores:
-        copy.wait()
+    reduce_wait(7)
+
+
+def final_kernel(y_in, a_hbm, b_hbm, y_hbm, a, b, y, in_sem, out_sem):
+    ab = [pltpu.make_async_copy(s, d, in_sem.at[i]) for i, (s, d) in enumerate(((a_hbm, a), (b_hbm, b)))]
+    ys = [pltpu.make_async_copy(y_in.at[pl.ds(r, n)], y.at[pl.ds(r, n)], in_sem.at[2 + i]) for i, (r, n, _) in enumerate(FIRST)]
+    outs = [pltpu.make_async_copy(y.at[pl.ds(r, n)], y_hbm.at[pl.ds(r, n)], out_sem.at[i]) for i, (r, n, _) in enumerate(FIRST + SECOND)]
+    for c in ab + ys:
+        c.start()
+    for c in ab:
+        c.wait()
+    for i, (at, (r, n, _)) in enumerate(zip(SECOND_AT, SECOND)):
+        y[pl.ds(r, n), :] = (a[pl.ds(at, n), :] + b[pl.ds(at, n), :]).astype(y.dtype)
+        outs[3 + i].start()
+    for i, c in enumerate(ys):
+        c.wait()
+        outs[i].start()
+    for c in outs:
+        c.wait()
 
 
 def solution(mesh):
@@ -295,11 +341,12 @@
         hbm = pl.BlockSpec(memory_space=pl.ANY)
         dma = pltpu.SemaphoreType.DMA
         f32, bf16 = jnp.float32, jnp.bfloat16
-        total, last = pl.pallas_call(
+        second = jax.ShapeDtypeStruct((SECOND_ROWS, hid), f32)
+        first, total, last = pl.pallas_call(
             moe_kernel,
-            out_shape=[jax.ShapeDtypeStruct((tok, hid), f32)] * 2,
+            out_shape=[jax.ShapeDtypeStruct((tok, hid), bf16), second, second],
             in_specs=[hbm] * 6,
-            out_specs=[hbm] * 2,
+            out_specs=[hbm] * 3,
             scratch_shapes=[
                 pltpu.VMEM((n_local, hid, ffn), bf16),
                 pltpu.VMEM((n_local, hid, ffn), bf16),
@@ -311,11 +358,11 @@
                 pltpu.VMEM((n_dev, 8, QUARTER), f32),
                 pltpu.VMEM((n_local, HALF, ffn), bf16),
                 pltpu.VMEM((8, tok, hid), f32),
-                pltpu.VMEM((6, tok, hid), f32),
+                pltpu.VMEM((7, tok, hid), f32),
                 pltpu.VMEM((2, HALF, hid), f32),
                 pltpu.VMEM((2, HALF, hid), f32),
                 dma((6,)), dma, dma((5,)), dma, dma((7,)), dma, dma((8,)),
-                dma, dma((7,)), dma((2,)), dma((2,)), pltpu.SemaphoreType.REGULAR((2,)),
+                dma, dma((8,)), dma((2,)), dma((2,)), pltpu.SemaphoreType.REGULAR((2,)),
             ],
             compiler_params=pltpu.CompilerParams(collective_id=0, has_side_effects=True, vmem_limit_bytes=66_000_000),
             name='moe_kernel',
@@ -323,11 +370,11 @@
         return pl.pallas_call(
             final_kernel,
             out_shape=jax.ShapeDtypeStruct((tok, hid), bf16),
-            in_specs=[hbm] * 2,
+            in_specs=[hbm] * 3,
             out_specs=hbm,
-            scratch_shapes=[pltpu.VMEM((tok, hid), f32), pltpu.VMEM((tok, hid), f32), pltpu.VMEM((tok, hid), bf16), dma((4, 2)), dma((4,))],
+            scratch_shapes=[pltpu.VMEM((SECOND_ROWS, hid), f32), pltpu.VMEM((SECOND_ROWS, hid), f32), pltpu.VMEM((tok, hid), bf16), dma((5,)), dma((8,))],
             name='final_kernel',
-        )(total, last)
+        )(first, total, last)
 
     tok_spec = P(TOKEN_AXES, None)
     w_spec = P(EXPERT_AXES, None, None)

time: 167 us -> 166 us (level)
  no operation moved by 1% of the time
where the time goes in v3:
time: 166 us
  Pallas kernels  166 us (100%)
    pallas_call x1, Pallas kernels, local_layer(): pl.pallas_call(moe_kernel, out_shape=[jax.ShapeDtypeStruct((tok, hid), bf...  164 us

profile of v3, /device:TPU:0, one launch (start us, length us, event | category | flops | bytes accessed | tf_op | source)
XLA Modules:
  0.0 166.1 jit_solution(11910871023223320527)
XLA Ops:
  0.0 163.8 %moe_kernel.1 = (bf16[512,1024]{1,0:T(8,128)(2,1)}, f32[128,1024]{1,0:T(8,128)}, f32[128,1024]{1,0:T(8,128)}) custom-call(bf16[512,1024]{1,0:T(8,128)(2,1)} %x_hbm.1, s32[8,512]{1,0:T(8,128)} %bitcast.2, f32[8,512]{1,0:T(8,128)} %bitcast.3, bf16[2,1024,512]{2,1,0:T(8,128)(2,1)} %w1_hbm.1, bf16[2,1024,512]{2,1,0:T(8,128)(2,1)} %w3_hbm.1, ...), custom_call_target="tpu_custom_call" | custom-call | tf_op jit(solution)/shard_map/moe_kernel/pallas_call | solution.py:345
  163.8 2.3 %final_kernel.1 = bf16[512,1024]{1,0:T(8,128)(2,1)} custom-call(bf16[512,1024]{1,0:T(8,128)(2,1)} %get-tuple-element.8.y_in, f32[128,1024]{1,0:T(8,128)} %get-tuple-element.9.a_hbm, f32[128,1024]{1,0:T(8,128)} %get-tuple-element.10.b_hbm), custom_call_target="tpu_custom_call" | custom-call | tf_op jit(solution)/shard_map/final_kernel/pallas_call | solution.py:370

commit v4 on v3

--- a/solution.py
+++ b/solution.py
@@ -31,9 +31,8 @@
     return masks(part).index(mask), masks(part).index(mask ^ axis), axis
 
 
-FIRST = [(r, 128, part) for part in PARTS[:3] for r in part[:1]]
+FIRST = [(part[0], 128, part) for part in PARTS[:3]]
 SECOND = [(part[0] + 128, 32, part) for part in PARTS[:3]] + [(part[0], part[1], part) for part in PARTS[3:]]
-SECOND_AT = (0, 32, 64, 96, 112)
 SECOND_ROWS = 128
 BITS = (2, 4, 8, 1)
 PATHS = {m: [b for b in BITS if m & b] for m in range(16)}
@@ -58,7 +57,7 @@
     return z, y, 2 * x + c
 
 
-def moe_kernel(x_hbm, ids_hbm, gates_hbm, w1_hbm, w3_hbm, w2_hbm, y_hbm, sum_hbm, last_hbm,
+def moe_kernel(x_hbm, ids_hbm, gates_hbm, w1_hbm, w3_hbm, w2_hbm, y_out,
                w1, w3, w2, ids, gates, x_all, tiles, merged, act, acc, rs, dd_out, dd_in,
                load_sem, gt_send, gt_recv, ag_send, ag_recv, xd_send, xd_recv,
                rs_send, rs_recv, dd_send, dd_recv, dd_free):
@@ -89,12 +88,11 @@
             remote(acc.at[w, rows], rs.at[k, rows], rs_send, rs_recv.at[k], axis).start()
 
     def reduce_last_start():
-        for r, n, part in FIRST:
-            w, _, axis = reduce_move(part, 6)
-            remote(acc.at[w, pl.ds(r, n)], rs.at[6, pl.ds(r, n)], rs_send, rs_recv.at[6], axis).start()
-        for at, (r, n, part) in zip(SECOND_AT, SECOND):
-            w, _, axis = reduce_move(part, 6)
-            remote(acc.at[w, pl.ds(r, n)], last_hbm.at[pl.ds(at, n)], rs_send, rs_recv.at[7], axis).start()
+        for i, piece in enumerate((FIRST, SECOND)):
+            for r, n, part in piece:
+                w, _, axis = reduce_move(part, 6)
+                rows = pl.ds(r, n)
+                remote(acc.at[w, rows], rs.at[6, rows], rs_send, rs_recv.at[6 + i], axis).start()
 
     def reduce_wait(k):
         rows = tok if k < 6 else SECOND_ROWS if k == 7 else tok - SECOND_ROWS
@@ -285,50 +283,23 @@
     add(4)
     reduce_last_start()
     add(5)
-    stores = [pltpu.make_async_copy(acc.at[0, pl.ds(r, n)], sum_hbm.at[pl.ds(at, n)], load_sem.at[i])
-              for i, (at, (r, n, _)) in enumerate(zip(SECOND_AT, SECOND))]
-    for c in stores:
-        c.start()
 
     drain(tiles.at[pl.ds(0, 2)], gt_send)
     drain(x_all.at[pl.ds(0, 7)], ag_send)
     drain(x_all.at[pl.ds(0, 8)], xd_send)
     for h in range(2):
         partial_copy(h).wait_send()
-    for c in stores:
-        c.wait()
+
+    def one(rows):
+        y_out[rows, :] = (acc[0, rows, :] + rs[6, rows, :]).astype(y_out.dtype)
 
     reduce_wait(6)
-    stores = []
-    for i, (r, n, _) in enumerate(FIRST):
-        def one(rows):
-            x_all[1, rows, :] = (acc[0, rows, :] + rs[6, rows, :]).astype(x_all.dtype)
-
+    for r, n, _ in FIRST:
         sum_rows(r, n, one)
-        stores.append(pltpu.make_async_copy(x_all.at[1, pl.ds(r, n)], y_hbm.at[pl.ds(r, n)], load_sem.at[i]))
-        stores[i].start()
-    for c in stores:
-        c.wait()
     drain(acc.at[pl.ds(0, 7)], rs_send)
     reduce_wait(7)
-
-
-def final_kernel(y_in, a_hbm, b_hbm, y_hbm, a, b, y, in_sem, out_sem):
-    ab = [pltpu.make_async_copy(s, d, in_sem.at[i]) for i, (s, d) in enumerate(((a_hbm, a), (b_hbm, b)))]
-    ys = [pltpu.make_async_copy(y_in.at[pl.ds(r, n)], y.at[pl.ds(r, n)], in_sem.at[2 + i]) for i, (r, n, _) in enumerate(FIRST)]
-    outs = [pltpu.make_async_copy(y.at[pl.ds(r, n)], y_hbm.at[pl.ds(r, n)], out_sem.at[i]) for i, (r, n, _) in enumerate(FIRST + SECOND)]
-    for c in ab + ys:
-        c.start()
-    for c in ab:
-        c.wait()
-    for i, (at, (r, n, _)) in enumerate(zip(SECOND_AT, SECOND)):
-        y[pl.ds(r, n), :] = (a[pl.ds(at, n), :] + b[pl.ds(at, n), :]).astype(y.dtype)
-        outs[3 + i].start()
-    for i, c in enumerate(ys):
-        c.wait()
-        outs[i].start()
-    for c in outs:
-        c.wait()
+    for r, n, _ in SECOND:
+        sum_rows(r, n, one)
 
 
 def solution(mesh):
@@ -341,12 +312,11 @@
         hbm = pl.BlockSpec(memory_space=pl.ANY)
         dma = pltpu.SemaphoreType.DMA
         f32, bf16 = jnp.float32, jnp.bfloat16
-        second = jax.ShapeDtypeStruct((SECOND_ROWS, hid), f32)
-        first, total, last = pl.pallas_call(
+        y = pl.pallas_call(
             moe_kernel,
-            out_shape=[jax.ShapeDtypeStruct((tok, hid), bf16), second, second],
+            out_shape=pltpu.VMEM((tok, hid), bf16),
             in_specs=[hbm] * 6,
-            out_specs=[hbm] * 3,
+            out_specs=pl.BlockSpec(memory_space=pltpu.VMEM),
             scratch_shapes=[
                 pltpu.VMEM((n_local, hid, ffn), bf16),
                 pltpu.VMEM((n_local, hid, ffn), bf16),
@@ -364,17 +334,10 @@
                 dma((6,)), dma, dma((5,)), dma, dma((7,)), dma, dma((8,)),
                 dma, dma((8,)), dma((2,)), dma((2,)), pltpu.SemaphoreType.REGULAR((2,)),
             ],
-            compiler_params=pltpu.CompilerParams(collective_id=0, has_side_effects=True, vmem_limit_bytes=66_000_000),
+            compiler_params=pltpu.CompilerParams(collective_id=0, has_side_effects=True, vmem_limit_bytes=62_000_000),
             name='moe_kernel',
         )(x_loc, ids_loc.T, gates_loc.T, w_g, w_u, w_d)
-        return pl.pallas_call(
-            final_kernel,
-            out_shape=jax.ShapeDtypeStruct((tok, hid), bf16),
-            in_specs=[hbm] * 3,
-            out_specs=hbm,
-            scratch_shapes=[pltpu.VMEM((SECOND_ROWS, hid), f32), pltpu.VMEM((SECOND_ROWS, hid), f32), pltpu.VMEM((tok, hid), bf16), dma((5,)), dma((8,))],
-            name='final_kernel',
-        )(first, total, last)
+        return y
 
     tok_spec = P(TOKEN_AXES, None)
     w_spec = P(EXPERT_AXES, None, None)

time: 166 us -> 165 us (level)
  Pallas kernels: 166 us -> 164 us
    pallas_call x2 -> x1, Pallas kernels: 166 us -> 164 us  [local_layer(): pl.pallas_call(moe_kernel, out_shape=pltpu.VMEM((tok, hid), bf16), in_spe...]
where the time goes in v4:
time: 165 us
  Pallas kernels  164 us (99%)
    pallas_call x1, Pallas kernels, local_layer(): pl.pallas_call(moe_kernel, out_shape=pltpu.VMEM((tok, hid), bf16), in_spe...  164 us

profile of v4, /device:TPU:0, one launch (start us, length us, event | category | flops | bytes accessed | tf_op | source)
XLA Modules:
  0.0 164.7 jit_solution(1812157628529941615)
XLA Ops:
  0.0 163.7 %moe_kernel.1 = bf16[512,1024]{1,0:T(8,128)(2,1)S(1)} custom-call(bf16[512,1024]{1,0:T(8,128)(2,1)} %x_hbm.1, s32[8,512]{1,0:T(8,128)} %bitcast.2, f32[8,512]{1,0:T(8,128)} %bitcast.3, bf16[2,1024,512]{2,1,0:T(8,128)(2,1)} %w1_hbm.1, bf16[2,1024,512]{2,1,0:T(8,128)(2,1)} %w3_hbm.1, bf16[2,512,1024]{2,1,0:T(8,128)(2,1)} %w2_hbm.1), custom_call_target="tpu_custom_call" | custom-call | tf_op jit(solution)/shard_map/moe_kernel/pallas_call | solution.py:315
  163.7 1.0 copy.8

commit v5 on v4

--- a/solution.py
+++ b/solution.py
@@ -281,8 +281,18 @@
     reduce_start(5)
     add(3)
     add(4)
-    reduce_last_start()
+    core = lax.axis_index('ex') % 2
+
+    @pl.when(core == 0)
+    def _():
+        reduce_last_start()
+
     add(5)
+
+    @pl.when(core == 1)
+    def _():
+        reduce_last_start()
+
 
     drain(tiles.at[pl.ds(0, 2)], gt_send)
     drain(x_all.at[pl.ds(0, 7)], ag_send)

time: 165 us -> 164 us (level)
  no operation moved by 1% of the time
where the time goes in v5:
time: 164 us
  Pallas kernels  163 us (99%)
    pallas_call x1, Pallas kernels, local_layer(): pl.pallas_call(moe_kernel, out_shape=pltpu.VMEM((tok, hid), bf16), in_spe...  163 us

profile of v5, /device:TPU:0, one launch (start us, length us, event | category | flops | bytes accessed | tf_op | source)
XLA Modules:
  0.0 163.9 jit_solution(14602915667918877864)
XLA Ops:
  0.0 162.9 %moe_kernel.1 = bf16[512,1024]{1,0:T(8,128)(2,1)S(1)} custom-call(bf16[512,1024]{1,0:T(8,128)(2,1)} %x_hbm.1, s32[8,512]{1,0:T(8,128)} %bitcast.2, f32[8,512]{1,0:T(8,128)} %bitcast.3, bf16[2,1024,512]{2,1,0:T(8,128)(2,1)} %w1_hbm.1, bf16[2,1024,512]{2,1,0:T(8,128)(2,1)} %w3_hbm.1, bf16[2,512,1024]{2,1,0:T(8,128)(2,1)} %w2_hbm.1), custom_call_target="tpu_custom_call" | custom-call | tf_op jit(solution)/shard_map/moe_kernel/pallas_call | solution.py:325
  162.9 1.0 copy.8

commit v6 on v5

--- a/solution.py
+++ b/solution.py
@@ -31,9 +31,9 @@
     return masks(part).index(mask), masks(part).index(mask ^ axis), axis
 
 
-FIRST = [(part[0], 128, part) for part in PARTS[:3]]
-SECOND = [(part[0] + 128, 32, part) for part in PARTS[:3]] + [(part[0], part[1], part) for part in PARTS[3:]]
-SECOND_ROWS = 128
+FIRST = [(part[0], 144, part) for part in PARTS[:3]]
+SECOND = [(part[0] + 144, 16, part) for part in PARTS[:3]] + [(part[0], part[1], part) for part in PARTS[3:]]
+SECOND_ROWS = 80
 BITS = (2, 4, 8, 1)
 PATHS = {m: [b for b in BITS if m & b] for m in range(16)}
 TILE_MOVES = (
@@ -79,7 +79,7 @@
         drain(x_all.at[2 * (k + 1)], ag_recv.at[k])
 
     def pair_copy(w):
-        return remote(x_all.at[2 * w], x_all.at[2 * w + 1], xd_send, xd_recv.at[w], 1)
+        return remote(x_all.at[2 * w], x_all.at[2 * w + 1], xd_send, xd_recv.at[w % 2], 1)
 
     def reduce_start(k, parts=PARTS):
         for part in parts:
@@ -109,8 +109,8 @@
         drain(tiles.at[0, pl.ds(0, len(TILE_MOVES[g]))], gt_recv.at[g])
 
     x_load = pltpu.make_async_copy(x_hbm, x_all.at[0], load_sem.at[0])
-    loads = [pltpu.make_async_copy(s, d, load_sem.at[1 + i]) for i, (s, d) in enumerate((
-        (ids_hbm, ids), (gates_hbm, gates), (w1_hbm, w1), (w3_hbm, w3), (w2_hbm, w2)))]
+    loads = [pltpu.make_async_copy(s, d, load_sem.at[i]) for i, s, d in (
+        (1, ids_hbm, ids), (1, gates_hbm, gates), (2, w1_hbm, w1), (2, w3_hbm, w3), (2, w2_hbm, w2))]
 
     barrier = pltpu.get_barrier_semaphore()
     for mask in BITS:
@@ -118,8 +118,7 @@
     x_load.start()
     for c in loads:
         c.start()
-    for c in loads[:2]:
-        c.wait()
+    drain(tiles.at[0, pl.ds(0, 8)], load_sem.at[1])
     for m in range(16):
         z, y, e = peer(m)
         for l in range(2):
@@ -136,8 +135,7 @@
     tiles_start(1)
     gather_start(1)
     gather_start(2)
-    for c in loads[2:]:
-        c.wait()
+    drain(x_all.at[pl.ds(0, 6)], load_sem.at[2])
 
     def merge_tiles(w):
         token = lax.broadcasted_iota(jnp.int32, (8, QUARTER), 0) // 2 * QUARTER + lax.broadcasted_iota(jnp.int32, (8, QUARTER), 1)
@@ -309,7 +307,7 @@
     drain(acc.at[pl.ds(0, 7)], rs_send)
     reduce_wait(7)
     for r, n, _ in SECOND:
-        sum_rows(r, n, one)
+        one(pl.ds(r, n))
 
 
 def solution(mesh):
@@ -341,7 +339,7 @@
                 pltpu.VMEM((7, tok, hid), f32),
                 pltpu.VMEM((2, HALF, hid), f32),
                 pltpu.VMEM((2, HALF, hid), f32),
-                dma((6,)), dma, dma((5,)), dma, dma((7,)), dma, dma((8,)),
+                dma((3,)), dma, dma((5,)), dma, dma((7,)), dma, dma((2,)),
                 dma, dma((8,)), dma((2,)), dma((2,)), pltpu.SemaphoreType.REGULAR((2,)),
             ],
             compiler_params=pltpu.CompilerParams(collective_id=0, has_side_effects=True, vmem_limit_bytes=62_000_000),

time: 164 us -> 164 us (level)
  no operation moved by 1% of the time
where the time goes in v6:
time: 164 us
  Pallas kernels  163 us (99%)
    pallas_call x1, Pallas kernels, local_layer(): pl.pallas_call(moe_kernel, out_shape=pltpu.VMEM((tok, hid), bf16), in_spe...  163 us

profile of v6, /device:TPU:0, one launch (start us, length us, event | category | flops | bytes accessed | tf_op | source)
XLA Modules:
  0.0 163.8 jit_solution(3490984468176779305)
XLA Ops:
  0.0 162.8 %moe_kernel.1 = bf16[512,1024]{1,0:T(8,128)(2,1)S(1)} custom-call(bf16[512,1024]{1,0:T(8,128)(2,1)} %x_hbm.1, s32[8,512]{1,0:T(8,128)} %bitcast.2, f32[8,512]{1,0:T(8,128)} %bitcast.3, bf16[2,1024,512]{2,1,0:T(8,128)(2,1)} %w1_hbm.1, bf16[2,1024,512]{2,1,0:T(8,128)(2,1)} %w3_hbm.1, bf16[2,512,1024]{2,1,0:T(8,128)(2,1)} %w2_hbm.1), custom_call_target="tpu_custom_call" | custom-call | tf_op jit(solution)/shard_map/moe_kernel/pallas_call | solution.py:323
  162.8 1.0 copy.8

commit v7 on v6

--- a/solution.py
+++ b/solution.py
@@ -37,8 +37,10 @@
 BITS = (2, 4, 8, 1)
 PATHS = {m: [b for b in BITS if m & b] for m in range(16)}
 TILE_MOVES = (
-    [(0, m) for m in range(1, 16)],
-    [(1, m) for m in range(16) if len(PATHS[m]) > 1],
+    [(0, 1)],
+    [(0, m) for m in range(2, 16)],
+    [(1, m) for m in (3, 5, 9)],
+    [(1, m) for m in (6, 7, 10, 11, 12, 13, 14, 15)],
     [(2, m) for m in (7, 11, 13)],
     [(2, m) for m in (14, 15)],
     [(3, 15)],
@@ -60,7 +62,7 @@
 def moe_kernel(x_hbm, ids_hbm, gates_hbm, w1_hbm, w3_hbm, w2_hbm, y_out,
                w1, w3, w2, ids, gates, x_all, tiles, merged, act, acc, rs, dd_out, dd_in,
                load_sem, gt_send, gt_recv, ag_send, ag_recv, xd_send, xd_recv,
-               rs_send, rs_recv, dd_send, dd_recv, dd_free):
+               rs_send, rs_recv, dd_send, dd_recv, dd_free, ready):
     tok = x_hbm.shape[0]
 
     def remote(src, dst, ssem, rsem, mask):
@@ -108,16 +110,47 @@
     def tiles_wait(g):
         drain(tiles.at[0, pl.ds(0, len(TILE_MOVES[g]))], gt_recv.at[g])
 
-    x_load = pltpu.make_async_copy(x_hbm, x_all.at[0], load_sem.at[0])
     loads = [pltpu.make_async_copy(s, d, load_sem.at[i]) for i, s, d in (
-        (1, ids_hbm, ids), (1, gates_hbm, gates), (2, w1_hbm, w1), (2, w3_hbm, w3), (2, w2_hbm, w2))]
-
+        (0, x_hbm, x_all.at[0]), (1, ids_hbm, ids), (1, gates_hbm, gates), (2, w1_hbm, w1), (2, w3_hbm, w3), (2, w2_hbm, w2))]
+
+    z, y, e = lax.axis_index('ez'), lax.axis_index('ey'), lax.axis_index('ex')
+    answers = {8: z, 4: y, 2: e // 2, 1: 1 - e % 2}
     barrier = pltpu.get_barrier_semaphore()
-    for mask in BITS:
-        pl.semaphore_signal(barrier, inc=1, device_id=peer(mask), device_id_type=MESH)
-    x_load.start()
+    for bit in BITS:
+        @pl.when(answers[bit] == 0)
+        def _(bit=bit):
+            pl.semaphore_signal(barrier, inc=1, device_id=peer(bit), device_id_type=MESH)
     for c in loads:
         c.start()
+    expected = z + y + e // 2 + 1 - e % 2
+
+    @pl.when(expected > 0)
+    def _():
+        pl.semaphore_wait(barrier, expected)
+
+    for i, bit in enumerate(BITS):
+        @pl.when(answers[bit] == 1)
+        def _(i=i, bit=bit):
+            pl.semaphore_signal(ready.at[i], inc=1, device_id=peer(bit), device_id_type=MESH)
+
+    def first_rows(bit):
+        for part in PARTS:
+            if part[2][0] == bit:
+                rows = pl.ds(part[0], part[1])
+                remote(x_hbm.at[rows], x_all.at[2, rows], ag_send, ag_recv.at[0], bit).start()
+        if bit == 1:
+            pair_copy(0).start()
+
+    for bit in BITS[:3]:
+        @pl.when(answers[bit] == 1)
+        def _(bit=bit):
+            first_rows(bit)
+    loads[0].wait()
+
+    @pl.when(answers[1] == 1)
+    def _():
+        first_rows(1)
+
     drain(tiles.at[0, pl.ds(0, 8)], load_sem.at[1])
     for m in range(16):
         z, y, e = peer(m)
@@ -126,16 +159,17 @@
             row = jnp.sum(jnp.where(hit, gates[...], 0.0), axis=0, keepdims=True)
             for q in range(4):
                 tiles[0, m, pl.ds(2 * q + l, 1), :] = row[:, q * QUARTER:(q + 1) * QUARTER]
-    x_load.wait()
-    pl.semaphore_wait(barrier, 4)
+    for i, bit in enumerate(BITS):
+        @pl.when(answers[bit] == 0)
+        def _(i=i, bit=bit):
+            pl.semaphore_wait(ready.at[i], 1)
+            first_rows(bit)
     tiles_start(0)
-    gather_start(0)
-    pair_copy(0).start()
-    tiles_wait(0)
     tiles_start(1)
     gather_start(1)
     gather_start(2)
     drain(x_all.at[pl.ds(0, 6)], load_sem.at[2])
+    tiles_wait(0)
 
     def merge_tiles(w):
         token = lax.broadcasted_iota(jnp.int32, (8, QUARTER), 0) // 2 * QUARTER + lax.broadcasted_iota(jnp.int32, (8, QUARTER), 1)
@@ -148,23 +182,16 @@
             merged[2 * w + side] = tile
 
     def before(j):
+        for g, onward in {1: ((1, (2, 3)),), 2: ((2, ()),), 7: ((3, (4, 5)),), 8: ((4, ()),), 13: ((5, (6,)),), 14: ((6, ()),)}.get(j, ()):
+            tiles_wait(g)
+            for k in onward:
+                tiles_start(k)
         if j % 2 == 1 and j < 14:
             w = (j + 1) // 2
             gather_wait(w - 1)
             for k in ONWARD[w - 1]:
                 gather_start(k)
             pair_copy(w).start()
-        if j == 1:
-            tiles_wait(1)
-            tiles_start(2)
-            tiles_start(3)
-        if j == 8:
-            tiles_wait(2)
-        if j == 13:
-            tiles_wait(3)
-            tiles_start(4)
-        if j == 14:
-            tiles_wait(4)
         if j % 2 == 0 and j < 16:
             merge_tiles(j // 2)
             pair_copy(j // 2).wait_recv()
@@ -339,8 +366,8 @@
                 pltpu.VMEM((7, tok, hid), f32),
                 pltpu.VMEM((2, HALF, hid), f32),
                 pltpu.VMEM((2, HALF, hid), f32),
-                dma((3,)), dma, dma((5,)), dma, dma((7,)), dma, dma((2,)),
-                dma, dma((8,)), dma((2,)), dma((2,)), pltpu.SemaphoreType.REGULAR((2,)),
+                dma((3,)), dma, dma((7,)), dma, dma((7,)), dma, dma((2,)),
+                dma, dma((8,)), dma((2,)), dma((2,)), pltpu.SemaphoreType.REGULAR((2,)), pltpu.SemaphoreType.REGULAR((4,)),
             ],
             compiler_params=pltpu.CompilerParams(collective_id=0, has_side_effects=True, vmem_limit_bytes=62_000_000),
             name='moe_kernel',

time: 164 us -> 163 us (level)
  Pallas kernels: 163 us -> 161 us
    pallas_call x1, Pallas kernels: 163 us -> 161 us  [local_layer(): pl.pallas_call(moe_kernel, out_shape=pltpu.VMEM((tok, hid), bf16), in_spe...]
where the time goes in v7:
time: 163 us; the launch traced here: 162 us
  Pallas kernels  161 us (99%)
    pallas_call x1, Pallas kernels, local_layer(): pl.pallas_call(moe_kernel, out_shape=pltpu.VMEM((tok, hid), bf16), in_spe...  161 us

profile of v7, /device:TPU:0, one launch (start us, length us, event | category | flops | bytes accessed | tf_op | source)
XLA Modules:
  0.0 161.7 jit_solution(17469995157529932679)
XLA Ops:
  0.0 160.7 %moe_kernel.1 = bf16[512,1024]{1,0:T(8,128)(2,1)S(1)} custom-call(bf16[512,1024]{1,0:T(8,128)(2,1)} %x_hbm.1, s32[8,512]{1,0:T(8,128)} %bitcast.2, f32[8,512]{1,0:T(8,128)} %bitcast.3, bf16[2,1024,512]{2,1,0:T(8,128)(2,1)} %w1_hbm.1, bf16[2,1024,512]{2,1,0:T(8,128)(2,1)} %w3_hbm.1, bf16[2,512,1024]{2,1,0:T(8,128)(2,1)} %w2_hbm.1), custom_call_target="tpu_custom_call" | custom-call | tf_op jit(solution)/shard_map/moe_kernel/pallas_call | solution.py:350
  160.8 1.0 copy.8

commit v8 on v7

--- a/solution.py
+++ b/solution.py
@@ -31,9 +31,9 @@
     return masks(part).index(mask), masks(part).index(mask ^ axis), axis
 
 
-FIRST = [(part[0], 144, part) for part in PARTS[:3]]
-SECOND = [(part[0] + 144, 16, part) for part in PARTS[:3]] + [(part[0], part[1], part) for part in PARTS[3:]]
-SECOND_ROWS = 80
+FIRST = [(part[0], 144, part) for part in PARTS[:3]] + [(part[0], part[1], part) for part in PARTS[3:]]
+SECOND = [(part[0] + 144, 16, part) for part in PARTS[:3]]
+SECOND_ROWS = 48
 BITS = (2, 4, 8, 1)
 PATHS = {m: [b for b in BITS if m & b] for m in range(16)}
 TILE_MOVES = (
@@ -61,7 +61,7 @@
 
 def moe_kernel(x_hbm, ids_hbm, gates_hbm, w1_hbm, w3_hbm, w2_hbm, y_out,
                w1, w3, w2, ids, gates, x_all, tiles, merged, act, acc, rs, dd_out, dd_in,
-               load_sem, gt_send, gt_recv, ag_send, ag_recv, xd_send, xd_recv,
+               load_sem, gt_send, gt_recv, ag_send, ag_recv, xd_recv,
                rs_send, rs_recv, dd_send, dd_recv, dd_free, ready):
     tok = x_hbm.shape[0]
 
@@ -81,24 +81,27 @@
         drain(x_all.at[2 * (k + 1)], ag_recv.at[k])
 
     def pair_copy(w):
-        return remote(x_all.at[2 * w], x_all.at[2 * w + 1], xd_send, xd_recv.at[w % 2], 1)
+        return remote(x_all.at[2 * w], x_all.at[2 * w + 1], ag_send, xd_recv.at[w % 2], 1)
+
+    def sum_sem(k):
+        return rs_recv.at[k] if k < 2 else ag_recv.at[k - 2] if k < 6 else gt_recv.at[k - 5]
 
     def reduce_start(k, parts=PARTS):
         for part in parts:
             w, _, axis = reduce_move(part, k)
             rows = pl.ds(part[0], part[1])
-            remote(acc.at[w, rows], rs.at[k, rows], rs_send, rs_recv.at[k], axis).start()
+            remote(acc.at[w, rows], rs.at[k, rows], rs_send, sum_sem(k), axis).start()
 
     def reduce_last_start():
         for i, piece in enumerate((FIRST, SECOND)):
             for r, n, part in piece:
                 w, _, axis = reduce_move(part, 6)
                 rows = pl.ds(r, n)
-                remote(acc.at[w, rows], rs.at[6, rows], rs_send, rs_recv.at[6 + i], axis).start()
+                remote(acc.at[w, rows], rs.at[6, rows], rs_send, sum_sem(6 + i), axis).start()
 
     def reduce_wait(k):
         rows = tok if k < 6 else SECOND_ROWS if k == 7 else tok - SECOND_ROWS
-        drain(acc.at[0, pl.ds(0, rows)], rs_recv.at[k])
+        drain(acc.at[0, pl.ds(0, rows)], sum_sem(k))
 
     def partial_copy(s):
         return remote(dd_out.at[s], dd_in.at[s], dd_send.at[s], dd_recv.at[s], 1)
@@ -320,8 +323,7 @@
 
 
     drain(tiles.at[pl.ds(0, 2)], gt_send)
-    drain(x_all.at[pl.ds(0, 7)], ag_send)
-    drain(x_all.at[pl.ds(0, 8)], xd_send)
+    drain(x_all.at[pl.ds(0, 15)], ag_send)
     for h in range(2):
         partial_copy(h).wait_send()
 
@@ -366,8 +368,8 @@
                 pltpu.VMEM((7, tok, hid), f32),
                 pltpu.VMEM((2, HALF, hid), f32),
                 pltpu.VMEM((2, HALF, hid), f32),
-                dma((3,)), dma, dma((7,)), dma, dma((7,)), dma, dma((2,)),
-                dma, dma((8,)), dma((2,)), dma((2,)), pltpu.SemaphoreType.REGULAR((2,)), pltpu.SemaphoreType.REGULAR((4,)),
+                dma((3,)), dma, dma((7,)), dma, dma((7,)), dma((2,)),
+                dma, dma((2,)), dma((2,)), dma((2,)), pltpu.SemaphoreType.REGULAR((2,)), pltpu.SemaphoreType.REGULAR((4,)),
             ],
             compiler_params=pltpu.CompilerParams(collective_id=0, has_side_effects=True, vmem_limit_bytes=62_000_000),
             name='moe_kernel',

time: 163 us -> 163 us (level)
  no operation moved by 1% of the time
where the time goes in v8:
time: 163 us; the launch traced here: 162 us
  Pallas kernels  161 us (99%)
    pallas_call x1, Pallas kernels, local_layer(): pl.pallas_call(moe_kernel, out_shape=pltpu.VMEM((tok, hid), bf16), in_spe...  161 us

profile of v8, /device:TPU:0, one launch (start us, length us, event | category | flops | bytes accessed | tf_op | source)
XLA Modules:
  0.0 161.7 jit_solution(4999642933874812454)
XLA Ops:
  0.0 160.7 %moe_kernel.1 = bf16[512,1024]{1,0:T(8,128)(2,1)S(1)} custom-call(bf16[512,1024]{1,0:T(8,128)(2,1)} %x_hbm.1, s32[8,512]{1,0:T(8,128)} %bitcast.2, f32[8,512]{1,0:T(8,128)} %bitcast.3, bf16[2,1024,512]{2,1,0:T(8,128)(2,1)} %w1_hbm.1, bf16[2,1024,512]{2,1,0:T(8,128)(2,1)} %w3_hbm.1, bf16[2,512,1024]{2,1,0:T(8,128)(2,1)} %w2_hbm.1), custom_call_target="tpu_custom_call" | custom-call | tf_op jit(solution)/shard_map/moe_kernel/pallas_call | solution.py:352
  160.7 1.0 copy.8

commit v9 on v8

--- a/solution.py
+++ b/solution.py
@@ -62,7 +62,7 @@
 def moe_kernel(x_hbm, ids_hbm, gates_hbm, w1_hbm, w3_hbm, w2_hbm, y_out,
                w1, w3, w2, ids, gates, x_all, tiles, merged, act, acc, rs, dd_out, dd_in,
                load_sem, gt_send, gt_recv, ag_send, ag_recv, xd_recv,
-               rs_send, rs_recv, dd_send, dd_recv, dd_free, ready):
+               rs_send, ready):
     tok = x_hbm.shape[0]
 
     def remote(src, dst, ssem, rsem, mask):
@@ -84,7 +84,7 @@
         return remote(x_all.at[2 * w], x_all.at[2 * w + 1], ag_send, xd_recv.at[w % 2], 1)
 
     def sum_sem(k):
-        return rs_recv.at[k] if k < 2 else ag_recv.at[k - 2] if k < 6 else gt_recv.at[k - 5]
+        return (gt_recv.at[0], ag_recv.at[0], ag_recv.at[1], ag_recv.at[2], ag_recv.at[3], gt_recv.at[3], gt_recv.at[1], gt_recv.at[2])[k]
 
     def reduce_start(k, parts=PARTS):
         for part in parts:
@@ -104,14 +104,14 @@
         drain(acc.at[0, pl.ds(0, rows)], sum_sem(k))
 
     def partial_copy(s):
-        return remote(dd_out.at[s], dd_in.at[s], dd_send.at[s], dd_recv.at[s], 1)
+        return remote(dd_out.at[s], dd_in.at[s], load_sem.at[2 + s], load_sem.at[s], 1)
 
     def tiles_start(g):
         for hop, m in TILE_MOVES[g]:
-            remote(tiles.at[hop, m], tiles.at[hop + 1, m], gt_send, gt_recv.at[g], PATHS[m][hop]).start()
+            remote(tiles.at[hop, m], tiles.at[hop + 1, m], gt_send, gt_recv.at[4 if g == 6 else g], PATHS[m][hop]).start()
 
     def tiles_wait(g):
-        drain(tiles.at[0, pl.ds(0, len(TILE_MOVES[g]))], gt_recv.at[g])
+        drain(tiles.at[0, pl.ds(0, len(TILE_MOVES[g]))], gt_recv.at[4 if g == 6 else g])
 
     loads = [pltpu.make_async_copy(s, d, load_sem.at[i]) for i, s, d in (
         (0, x_hbm, x_all.at[0]), (1, ids_hbm, ids), (1, gates_hbm, gates), (2, w1_hbm, w1), (2, w3_hbm, w3), (2, w2_hbm, w2))]
@@ -255,7 +255,7 @@
 
             @pl.when(i >= 2)
             def _():
-                pl.semaphore_wait(dd_free.at[h], 1)
+                pl.semaphore_wait(ready.at[3 * h], 1)
 
             partial_copy(h).start()
 
@@ -273,7 +273,7 @@
 
             @pl.when(i < 15)
             def _():
-                pl.semaphore_signal(dd_free.at[h], inc=1, device_id=peer(1), device_id_type=MESH)
+                pl.semaphore_signal(ready.at[3 * h], inc=1, device_id=peer(1), device_id_type=MESH)
 
         for j in (7, 10):
             @pl.when(i == j)
@@ -368,8 +368,8 @@
                 pltpu.VMEM((7, tok, hid), f32),
                 pltpu.VMEM((2, HALF, hid), f32),
                 pltpu.VMEM((2, HALF, hid), f32),
-                dma((3,)), dma, dma((7,)), dma, dma((7,)), dma((2,)),
-                dma, dma((2,)), dma((2,)), dma((2,)), pltpu.SemaphoreType.REGULAR((2,)), pltpu.SemaphoreType.REGULAR((4,)),
+                dma((4,)), dma, dma((6,)), dma, dma((7,)), dma((2,)),
+                dma, pltpu.SemaphoreType.REGULAR((4,)),
             ],
             compiler_params=pltpu.CompilerParams(collective_id=0, has_side_effects=True, vmem_limit_bytes=62_000_000),
             name='moe_kernel',

time: 163 us -> 162 us (level)
  no operation moved by 1% of the time
where the time goes in v9:
time: 162 us
  Pallas kernels  161 us (99%)
    pallas_call x1, Pallas kernels, local_layer(): pl.pallas_call(moe_kernel, out_shape=pltpu.VMEM((tok, hid), bf16), in_spe...  161 us

profile of v9, /device:TPU:0, one launch (start us, length us, event | category | flops | bytes accessed | tf_op | source)
XLA Modules:
  0.0 161.6 jit_solution(3432675129974078423)
XLA Ops:
  0.0 160.6 %moe_kernel.1 = bf16[512,1024]{1,0:T(8,128)(2,1)S(1)} custom-call(bf16[512,1024]{1,0:T(8,128)(2,1)} %x_hbm.1, s32[8,512]{1,0:T(8,128)} %bitcast.2, f32[8,512]{1,0:T(8,128)} %bitcast.3, bf16[2,1024,512]{2,1,0:T(8,128)(2,1)} %w1_hbm.1, bf16[2,1024,512]{2,1,0:T(8,128)(2,1)} %w3_hbm.1, bf16[2,512,1024]{2,1,0:T(8,128)(2,1)} %w2_hbm.1), custom_call_target="tpu_custom_call" | custom-call | tf_op jit(solution)/shard_map/moe_kernel/pallas_call | solution.py:352
  160.6 1.0 copy.8

commit v10 on v9

--- a/solution.py
+++ b/solution.py
@@ -75,10 +75,13 @@
         w, a = GATHER[k]
         for part in PARTS:
             rows = pl.ds(part[0], part[1])
-            remote(x_all.at[2 * w, rows], x_all.at[2 * (k + 1), rows], ag_send, ag_recv.at[k], part[2][a]).start()
+            remote(x_all.at[2 * w, rows], x_all.at[2 * (k + 1), rows], ag_send, ag_recv.at[min(k, 4) if k < 6 else 5], part[2][a]).start()
 
     def gather_wait(k):
-        drain(x_all.at[2 * (k + 1)], ag_recv.at[k])
+        if k == 4:
+            drain(x_all.at[pl.ds(0, 2)], ag_recv.at[4])
+        elif k != 5:
+            drain(x_all.at[2 * (k + 1)], ag_recv.at[min(k, 5)])
 
     def pair_copy(w):
         return remote(x_all.at[2 * w], x_all.at[2 * w + 1], ag_send, xd_recv.at[w % 2], 1)
@@ -368,7 +371,7 @@
                 pltpu.VMEM((7, tok, hid), f32),
                 pltpu.VMEM((2, HALF, hid), f32),
                 pltpu.VMEM((2, HALF, hid), f32),
-                dma((4,)), dma, dma((6,)), dma, dma((7,)), dma((2,)),
+                dma((4,)), dma, dma((6,)), dma, dma((6,)), dma((2,)),
                 dma, pltpu.SemaphoreType.REGULAR((4,)),
             ],
             compiler_params=pltpu.CompilerParams(collective_id=0, has_side_effects=True, vmem_limit_bytes=62_000_000),

time: 162 us -> 162 us (level)
  no operation moved by 1% of the time
where the time goes in v10:
time: 162 us
  Pallas kernels  161 us (99%)
    pallas_call x1, Pallas kernels, local_layer(): pl.pallas_call(moe_kernel, out_shape=pltpu.VMEM((tok, hid), bf16), in_spe...  161 us

profile of v10, /device:TPU:0, one launch (start us, length us, event | category | flops | bytes accessed | tf_op | source)
XLA Modules:
  0.0 161.8 jit_solution(18120975654034016691)
XLA Ops:
  0.0 160.8 %moe_kernel.1 = bf16[512,1024]{1,0:T(8,128)(2,1)S(1)} custom-call(bf16[512,1024]{1,0:T(8,128)(2,1)} %x_hbm.1, s32[8,512]{1,0:T(8,128)} %bitcast.2, f32[8,512]{1,0:T(8,128)} %bitcast.3, bf16[2,1024,512]{2,1,0:T(8,128)(2,1)} %w1_hbm.1, bf16[2,1024,512]{2,1,0:T(8,128)(2,1)} %w3_hbm.1, bf16[2,512,1024]{2,1,0:T(8,128)(2,1)} %w2_hbm.1), custom_call_target="tpu_custom_call" | custom-call | tf_op jit(solution)/shard_map/moe_kernel/pallas_call | solution.py:355
  160.8 1.0 copy.8

commit v11 on v10

--- a/solution.py
+++ b/solution.py
@@ -107,7 +107,7 @@
         drain(acc.at[0, pl.ds(0, rows)], sum_sem(k))
 
     def partial_copy(s):
-        return remote(dd_out.at[s], dd_in.at[s], load_sem.at[2 + s], load_sem.at[s], 1)
+        return remote(dd_out.at[s], dd_in.at[s], load_sem.at[2], load_sem.at[s], 1)
 
     def tiles_start(g):
         for hop, m in TILE_MOVES[g]:
@@ -245,7 +245,7 @@
             w, h = i // 2, i % 2
             rows = pl.ds(pl.multiple_of(h * HALF, HALF), HALF)
 
-            @pl.when(i >= 2)
+            @pl.when(i >= 1)
             def _():
                 partial_copy(h).wait_send()
 
@@ -327,8 +327,7 @@
 
     drain(tiles.at[pl.ds(0, 2)], gt_send)
     drain(x_all.at[pl.ds(0, 15)], ag_send)
-    for h in range(2):
-        partial_copy(h).wait_send()
+    partial_copy(0).wait_send()
 
     def one(rows):
         y_out[rows, :] = (acc[0, rows, :] + rs[6, rows, :]).astype(y_out.dtype)
@@ -371,7 +370,7 @@
                 pltpu.VMEM((7, tok, hid), f32),
                 pltpu.VMEM((2, HALF, hid), f32),
                 pltpu.VMEM((2, HALF, hid), f32),
-                dma((4,)), dma, dma((6,)), dma, dma((6,)), dma((2,)),
+                dma((3,)), dma, dma((6,)), dma, dma((6,)), dma((2,)),
                 dma, pltpu.SemaphoreType.REGULAR((4,)),
             ],
             compiler_params=pltpu.CompilerParams(collective_id=0, has_side_effects=True, vmem_limit_bytes=62_000_000),

time: 162 us -> 162 us (level)
  no operation moved by 1% of the time
where the time goes in v11:
time: 162 us
  Pallas kernels  161 us (99%)
    pallas_call x1, Pallas kernels, local_layer(): pl.pallas_call(moe_kernel, out_shape=pltpu.VMEM((tok, hid), bf16), in_spe...  161 us

profile of v11, /device:TPU:0, one launch (start us, length us, event | category | flops | bytes accessed | tf_op | source)
XLA Modules:
  0.0 162.2 jit_solution(11220684219967901602)
XLA Ops:
  0.0 161.2 %moe_kernel.1 = bf16[512,1024]{1,0:T(8,128)(2,1)S(1)} custom-call(bf16[512,1024]{1,0:T(8,128)(2,1)} %x_hbm.1, s32[8,512]{1,0:T(8,128)} %bitcast.2, f32[8,512]{1,0:T(8,128)} %bitcast.3, bf16[2,1024,512]{2,1,0:T(8,128)(2,1)} %w1_hbm.1, bf16[2,1024,512]{2,1,0:T(8,128)(2,1)} %w3_hbm.1, bf16[2,512,1024]{2,1,0:T(8,128)(2,1)} %w2_hbm.1), custom_call_target="tpu_custom_call" | custom-call | tf_op jit(solution)/shard_map/moe_kernel/pallas_call | solution.py:354
  161.2 1.0 copy.8
